TPU v7x, 128 devices: a whole 4x4x4 slice. The times are simulated.
128 devices in a mesh: tile: 8 (over y, core), slab: 16 (over z, x).
Axes of the slice: x: 4, y: 4, z: 4, core: 2. Of those that a mesh axis runs over, the one named last changes fastest.
Arguments:
- volume: float32 [512, 32768], P('slab', 'tile'), may hold values from -6 to 6
- measured: float32 [512, 8192], P('slab', 'tile'), may hold values from -6 to 6
- weights: float32 [512, 8192], P('slab', 'tile'), may hold values from 0.25 to 4
- footprints: float32 [2048, 32, 128], P('tile'), may hold values from -0.1875 to 0.1875
- foot_pixel: int32 [2048], P('tile'), may hold values from 0 to 31
- foot_strip: int32 [2048], P('tile'), may hold values from 0 to 255
Outputs:
- smoothed: float32 [512, 32768], P('slab', 'tile')
- residual: float32 [512, 8192], P('slab', 'tile')
Inputs may be any that keep to these rules, and one draw needn't show every extreme that they name: foot_pixel names one of the 32 pixel blocks of the tile that holds the footprint block. foot_strip names a strip of 32 rays.
All inputs are finite; a program needn't handle non-finite values.
Results may differ from a plain program's by a relative error of at most 0.0003.
Values sent between devices are 32-bit elements; how exact they have to be, the bound alone decides.
No kernel may reach another device: no remote copies, remote signals or barrier semaphores. Data moves between devices by JAX's collectives and lax.ppermute only.
A program may use at most 64 MiB of HBM per device.

v0:
```python
import jax
import jax.numpy as jnp
from jax import lax
from jax.experimental import pallas as pl
from jax.experimental.pallas import tpu as pltpu
from jax.sharding import Mesh
from jax.sharding import PartitionSpec as P


PASSES = 3
TILE = ("tile_0", "tile_1")
SLAB = ("slab_0", "slab_1")
GROUP = 4
UNROLL = 32
CHUNKS = 4

huber_width = 0.5
smooth_rate = 0.2


VM = pl.BlockSpec(memory_space=pltpu.VMEM)
SM = pl.BlockSpec(memory_space=pltpu.SMEM)
AN = pl.BlockSpec(memory_space=pltpu.HBM)
F32 = jnp.float32
BF16 = jnp.bfloat16


def call(kernel, outs, ins, scratch=(), smem=0, flops=1000000, limit=24, any_at=()):
    specs = [AN if n in any_at else SM if n < smem else VM for n in range(len(ins))]
    return pl.pallas_call(
        kernel,
        out_shape=[s if hasattr(s, "dtype") else jax.ShapeDtypeStruct(s, F32) for s in outs],
        in_specs=specs,
        out_specs=[VM] * len(outs),
        scratch_shapes=list(scratch),
        compiler_params=pltpu.CompilerParams(vmem_limit_bytes=limit << 20),
        cost_estimate=pl.CostEstimate(flops=flops, bytes_accessed=1 << 20, transcendentals=0),
    )(*ins)


def halves(value):
    high = value.astype(BF16)
    return high, (value - high.astype(F32)).astype(BF16)


def lane_groups(shape):
    return lax.broadcasted_iota(jnp.int32, shape, 1) // 32


def place(spots, b):
    pixels, strips, me = spots
    strip = strips[b]
    owner = strip >> 5
    slot = (((owner & 1) ^ me[1]) << 2) | (((owner >> 1) - me[0]) & 3)
    return (slot << 3) | ((strip >> 2) & 7), strip & 3, pixels[b]


def stacked(pair):
    high = pair[:, :128]
    return jnp.concatenate([pair, jnp.concatenate([high, jnp.zeros_like(high)], axis=1)], axis=0)


def forward_step(spots, g, pair, high, low, rays, groups):
    where = [place(spots, GROUP * g + i) for i in range(GROUP)]
    left = jnp.concatenate([jnp.concatenate([high[w[2]], low[w[2]]], axis=1) for w in where], axis=0)
    both = lax.dot_general(left, stacked(pair), (((1,), (0,)), ((), ())), preferred_element_type=F32)
    product = both[:, :128] + both[:, 128:]
    for i, (entry, spot, _) in enumerate(where):
        own = jnp.where(groups == i, product[32 * i : 32 * i + 32], 0.0)
        rays[entry] += pltpu.roll(own, ((spot - i) & 3) * 32, 1)


def forward_loop(spots, turned, high, low, rays):
    rays[...] = jnp.zeros_like(rays)
    groups = lane_groups((32, 128))

    def step(g, carry):
        forward_step(spots, g, turned[g], high, low, rays, groups)
        return carry

    lax.fori_loop(0, turned.shape[0], step, 0, unroll=UNROLL)


def back_loop(spots, plain, rays, field):
    field[...] = jnp.zeros_like(field)
    groups = lane_groups((32, 128))

    def step(g, carry):
        where = [place(spots, GROUP * g + i) for i in range(GROUP)]
        rows = []
        for i, (entry, spot, _) in enumerate(where):
            turned = pltpu.roll(rays[entry], ((i - spot) & 3) * 32, 1)
            own = jnp.where(groups == i, turned, 0.0)
            rows.append(jnp.concatenate(halves(own), axis=1))
        left = jnp.concatenate(rows, axis=0)
        both = lax.dot_general(
            left, stacked(plain[g]), (((1,), (0,)), ((), ())), preferred_element_type=F32
        )
        product = both[:, :128] + both[:, 128:]
        for i, (_, _, pixel) in enumerate(where):
            field[pixel] += product[32 * i : 32 * i + 32]
        return carry

    lax.fori_loop(0, plain.shape[0], step, 0, unroll=UNROLL)


def hand_out(rays, mine, theirs):
    mine[...] = rays[:32].reshape(mine.shape)
    theirs[...] = rays[32:].reshape(theirs.shape)


def first_kernel(pixels_hbm, strips_hbm, me, foot_hbm, volume_hbm, *refs):
    mine, theirs, first, last, plain, turned, foot, volume, high, low, rays, pixels, strips, sem, foot_sem = refs
    spots = (pixels, strips, me)
    per = foot.shape[0] // CHUNKS

    def chunk(t):
        some = pl.ds(t * per, per)
        return pltpu.make_async_copy(foot_hbm.at[some], foot.at[some], foot_sem.at[t])

    field = pltpu.make_async_copy(volume_hbm, volume, sem.at[0])
    field.start()
    indices = [
        pltpu.make_async_copy(pixels_hbm, pixels, sem.at[1]),
        pltpu.make_async_copy(strips_hbm, strips, sem.at[2]),
    ]
    for copy in indices:
        copy.start()
    for t in range(CHUNKS):
        chunk(t).start()
    rays[...] = jnp.zeros_like(rays)
    groups = lane_groups((32, 128))
    for copy in (*indices, field):
        copy.wait()
    for p in range(high.shape[0]):
        cols = slice(128 * p, 128 * p + 128)
        high[p], low[p] = halves(volume[:, cols])
        first[p], last[p] = volume[0:8, cols], volume[24:32, cols]

    def trip(t, carry):
        chunk(t).wait()
        for u in range(per // GROUP):
            g = t * (per // GROUP) + u
            block = foot[pl.ds(GROUP * g, GROUP)].reshape(GROUP * 32, 128)
            plain[g] = jnp.concatenate(halves(block), axis=1)
            pair = jnp.concatenate(halves(block.T), axis=1)
            turned[g] = pair
            forward_step(spots, g, pair, high, low, rays, groups)
        return carry

    lax.fori_loop(0, CHUNKS, trip, 0)
    hand_out(rays, mine, theirs)


def folded(value):
    return jnp.sum(value.reshape(-1, 8, 128), axis=0)


def there_and_back(spots, plain, turned, pieces, mine, theirs, field, high, low, rays):
    for slot, piece in enumerate(pieces):
        rays[8 * slot : 8 * slot + 8] = piece[...]
    back_loop(spots, plain, rays, field)
    for p in range(high.shape[0]):
        high[p], low[p] = halves(field[p])
    forward_loop(spots, turned, high, low, rays)
    hand_out(rays, mine, theirs)


def second_kernel(pixels, strips, me, plain, turned, *refs):
    pieces, (mine, theirs, field, sums, high, low, rays) = refs[:8], refs[8:]
    there_and_back((pixels, strips, me), plain, turned, pieces, mine, theirs, field, high, low, rays)
    sums[0] = folded(field[...] * field[...])


def third_kernel(pixels, strips, me, plain, turned, *refs):
    pieces, grad = refs[:8], refs[8]
    mine, theirs, field, sums, first, last, high, low, rays = refs[9:]
    there_and_back((pixels, strips, me), plain, turned, pieces, mine, theirs, field, high, low, rays)
    sums[0] = folded(grad[...] * field[...])
    sums[1] = folded(field[...] * field[...])
    row = lax.broadcasted_iota(jnp.int32, (8, 128), 0)
    for p in range(field.shape[0]):
        first[p] = jnp.where(row < 3, grad[p, 0:8], pltpu.roll(field[p, 0:8], 3, 0))
        last[p] = jnp.where(row > 4, grad[p, 24:32], pltpu.roll(field[p, 24:32], 5, 0))


def add_kernel(mine, got, kept, s1, s2, s3):
    for r, out in enumerate((kept, s1, s2, s3)):
        out[...] = mine[r] + got[r]


def tile_cols(ref):
    return jnp.stack([ref[:, 128 * t : 128 * t + 128] for t in range(ref.shape[1] // 128)])


def start_kernel(kept, a, b, c, measured, weights, residual, sent):
    value = kept[...] + a[...] + b[...] + c[...] - tile_cols(measured)
    residual[...] = value
    sent[...] = tile_cols(weights) * value


def middle_kernel(kept, a, b, c, weights, projected, sent, sums):
    value = kept[...] + a[...] + b[...] + c[...]
    weighted = tile_cols(weights) * value
    projected[...] = value
    sent[...] = weighted
    sums[0] = folded(weighted * value)


def in_lanes(sums, shape):
    lane = lax.broadcasted_iota(jnp.int32, shape, 1)
    value = jnp.zeros(shape, F32)
    for n, part in enumerate(sums):
        value = jnp.where(lane == n, jnp.sum(part, keepdims=True), value)
    return value


def end_kernel(kept, a, b, c, weights, before, norm0, curve0, turned, projected, rows):
    value = kept[...] + a[...] + b[...] + c[...]
    weighted = tile_cols(weights) * value
    projected[...] = value
    cross = folded(weighted * before[...])
    rows[...] = in_lanes([norm0[0], curve0[0], turned[0], turned[1], cross, folded(weighted * value)], rows.shape)


def totals(rows, count):
    value = jnp.sum(rows[...], axis=0, keepdims=True)
    return [value[:, n : n + 1] for n in range(count)]


def scalar(value):
    return jnp.sum(value)


def judge_kernel(rows, alphas, again):
    norm0, curve0, cross_g, square_g, cross_p, square_p = totals(rows, 6)
    alpha = norm0 / curve0
    norm1 = norm0 - 2.0 * alpha * cross_g + alpha * alpha * square_g
    curve1 = curve0 - 2.0 * alpha * cross_p + alpha * alpha * square_p
    sound = (norm1 > 0.01 * norm0) & (curve1 > 0.01 * curve0)
    for square in (square_g, square_p):
        sound = sound & (square > 1e-25) & (square < 1e37)
    alphas[0] = scalar(alpha)
    alphas[1] = scalar(norm1 / curve1)
    again[0] = jnp.where(scalar(jnp.where(sound, F32(0.0), F32(1.0))) > 0.5, 1, 0)


def again_kernel(alphas, weights, p0, q0, grad, turned, rows):
    value = p0[...] - alphas[0] * q0[...]
    step = grad[...] - alphas[0] * turned[...]
    rows[...] = in_lanes([folded(step * step), folded(tile_cols(weights) * value * value)], rows.shape)


def ratio_kernel(alphas, rows, out):
    norm1, curve1 = totals(rows, 2)
    out[0] = alphas[0]
    out[1] = scalar(norm1 / curve1)


def smooth_kernel(ends, alphas, volume, grad, turned, first0, last0, first, last, residual, p0, q0, smoothed, left_over):
    alpha0, alpha1 = alphas[0], alphas[1]
    rest = residual[...] - alpha0 * p0[...] - alpha1 * (p0[...] - alpha0 * q0[...])
    for t in range(rest.shape[0]):
        left_over[:, 128 * t : 128 * t + 128] = rest[t]

    def stepped(x, g, h):
        return x - alpha0 * g - alpha1 * (g - alpha0 * h)

    row = lax.broadcasted_iota(jnp.int32, (48, 128), 0)
    open_link = ~(((row == 7) & (ends[0] == 1)) | ((row == 39) & (ends[1] == 1)))
    link = jnp.where(open_link, F32(1.0), F32(0.0))
    for p in range(grad.shape[0]):
        cols = slice(128 * p, 128 * p + 128)
        ext = jnp.concatenate(
            [
                stepped(last0[p], last[p], pltpu.roll(last[p], 3, 0)),
                stepped(volume[:, cols], grad[p], turned[p]),
                stepped(first0[p], first[p], pltpu.roll(first[p], 5, 0)),
            ],
            axis=0,
        )
        for _ in range(PASSES):
            clipped = jnp.clip(pltpu.roll(ext, 47, 0) - ext, -huber_width, huber_width) * link
            ext = ext + smooth_rate * (clipped - pltpu.roll(clipped, 1, 0))
        smoothed[:, cols] = ext[8:40]


def shift(value, axis, by):
    n = lax.axis_size(axis)
    return lax.ppermute(value, axis, [(i, (i + by) % n) for i in range(n)])


RAY = (8, 32, 128)


def summed_by_owner(mine, theirs):
    got = shift(theirs, "tile_1", 1)
    kept, s1, s2, s3 = call(add_kernel, [RAY] * 4, [mine, got])
    return kept, shift(s1, "tile_0", 1), shift(s2, "tile_0", 2), shift(s3, "tile_0", 3)


def to_everyone(own):
    column = [own] + [shift(own, "tile_0", -r) for r in (1, 2, 3)]
    return column + [shift(block, "tile_1", 1) for block in column]


def over_all(rows):
    return lax.all_to_all(rows, TILE + SLAB, 0, 0, tiled=True)


def shards(volume, measured, weights, footprints, foot_pixel, foot_strip):
    me = jnp.stack([lax.axis_index("tile_0"), lax.axis_index("tile_1")])
    spots = [foot_pixel, foot_strip, me]
    slabs = lax.axis_size(SLAB)
    place_in = lax.axis_index(SLAB)
    ends = jnp.stack([place_in == 0, place_in == slabs - 1]).astype(jnp.int32)
    up = [(i, (i + 1) % slabs) for i in range(slabs)]
    down = [(j, i) for i, j in up]

    field, tile = (32, 32, 128), (1, 8, 128)
    scratch = [pltpu.VMEM(field, BF16), pltpu.VMEM(field, BF16), pltpu.VMEM((64, 32, 128), F32)]
    in_place = [pltpu.with_memory_space_constraint(x, pltpu.HBM) for x in (foot_pixel, foot_strip, footprints, volume)]
    streams = [
        pltpu.VMEM(footprints.shape, F32),
        pltpu.VMEM(volume.shape, F32),
        *scratch,
        pltpu.SMEM(foot_pixel.shape, jnp.int32),
        pltpu.SMEM(foot_strip.shape, jnp.int32),
        pltpu.SemaphoreType.DMA((3,)),
        pltpu.SemaphoreType.DMA((CHUNKS,)),
    ]
    split = jax.ShapeDtypeStruct((64, 128, 256), BF16)
    half, edge = (4,) + RAY, (32, 8, 128)
    mine, theirs, first0, last0, plain, turned = call(
        first_kernel,
        [half, half, edge, edge, split, split],
        [*in_place[:2], me, *in_place[2:]],
        streams,
        3,
        any_at=(0, 1, 3, 4),
        limit=32,
    )
    parts = summed_by_owner(mine, theirs)
    residual, sent = call(start_kernel, [RAY, RAY], [*parts, measured, weights])

    mine, theirs, grad, norm0 = call(
        second_kernel, [half, half, field, tile], [*spots, plain, turned, *to_everyone(sent)], scratch, 3
    )
    mine, theirs, first0, last0 = lax.optimization_barrier((mine, theirs, first0, last0))
    parts = summed_by_owner(mine, theirs)
    first0, last0 = lax.ppermute(first0, SLAB, down), lax.ppermute(last0, SLAB, up)
    parts, first0, last0 = lax.optimization_barrier((parts, first0, last0))
    p0, sent, curve0 = call(middle_kernel, [RAY, RAY, tile], [*parts, weights])

    mine, theirs, back, crossed, first, last = call(
        third_kernel,
        [half, half, field, (2, 8, 128), edge, edge],
        [*spots, plain, turned, *to_everyone(sent), grad],
        scratch,
        3,
    )
    parts = summed_by_owner(mine, theirs)
    first, last = lax.ppermute(first, SLAB, down), lax.ppermute(last, SLAB, up)
    everyone = slabs * lax.axis_size(TILE)
    q0, rows = call(
        end_kernel, [RAY, (everyone, 128)], [*parts, weights, p0, norm0, curve0, crossed]
    )
    rows, first, last, ends = lax.optimization_barrier((rows, first, last, ends))
    rows = over_all(rows)
    alphas, again = pl.pallas_call(
        judge_kernel,
        out_shape=[jax.ShapeDtypeStruct((2,), F32), jax.ShapeDtypeStruct((1,), jnp.int32)],
        in_specs=[VM],
        out_specs=[SM, SM],
        compiler_params=pltpu.CompilerParams(vmem_limit_bytes=8 << 20),
    )(rows)

    def summed_again(alphas):
        rows = call(again_kernel, [(everyone, 128)], [alphas, weights, p0, q0, grad, back], (), 1)[0]
        return pl.pallas_call(
            ratio_kernel,
            out_shape=jax.ShapeDtypeStruct((2,), F32),
            in_specs=[SM, VM],
            out_specs=SM,
            compiler_params=pltpu.CompilerParams(vmem_limit_bytes=8 << 20),
        )(alphas, over_all(rows))

    alphas = lax.cond(again[0] == 1, summed_again, lambda known: known, alphas)
    return call(
        smooth_kernel,
        [volume.shape, measured.shape],
        [ends, alphas, volume, grad, back, first0, last0, first, last, residual, p0, q0],
        (),
        2,
    )


def solution(mesh):
    finer = Mesh(mesh.devices.reshape(4, 2, 4, 4), ("tile_0", "tile_1", "slab_0", "slab_1"))
    return jax.shard_map(
        lambda *args: tuple(shards(*args)),
        mesh=finer,
        in_specs=(
            P(SLAB, TILE),
            P(SLAB, TILE),
            P(SLAB, TILE),
            P(TILE, None, None),
            P(TILE),
            P(TILE),
        ),
        out_specs=(P(SLAB, TILE), P(SLAB, TILE)),
        check_vma=False,
    )
```

profile of v0, /device:TPU:1, one launch (start us, length us, event | category | flops | bytes accessed | tf_op | source)
XLA Modules:
  0.0 108.1 jit_solution(11169781108804043468)
XLA Ops:
  0.8 5.7 %shard_map.77 = (f32[4,8,32,128]{3,2,1,0:T(8,128)S(1)}, f32[4,8,32,128]{3,2,1,0:T(8,128)S(1)}, f32[32,8,128]{2,1,0:T(8,128)S(1)}, f32[32,8,128]{2,1,0:T(8,128)S(...) custom-call(s32[256]{0:T(256)} %pixels.3, s32[256]{0:T(256)} %strips.3, s32[2]{0:T(128)S(1)} %pad_add_fusion.me, ...), custom_call_target="tpu_custom_call" | custom-call | flops 1000000 | bytes 1048576 | tf_op jit(solution)/shard_map/pallas_call | solution.py:30
  6.5 1.5 %collective-permute-start = (f32[4,8,32,128]{3,2,1,0:T(8,128)S(1)}, f32[4,8,32,128]{3,2,1,0:T(8,128)S(1)}, u32[]{:S(2)}, u32[]{:S(2)}) collective-permute-start(f32[4,8,32,128]{3,2,1,0:T(8,128)S(1)} %get-tuple-element.78), channel_id=1, source_target_pairs={{0,16},{16,0},{1,17},{17,1},{2,18},{18,2},{3,19},{19,3},{4,20},{20... | collective-permute-start | bytes 1572872 | tf_op jit(solution)/shard_map/ppermute | solution.py:290
  8.0 1.5 %collective-permute-done.got = f32[4,8,32,128]{3,2,1,0:T(8,128)S(1)} collective-permute-done((f32[4,8,32,128]{3,2,1,0:T(8,128)S(1)}, f32[4,8,32,128]{3,2,1,0:T(8,128)S(1)}, u32[]{:S(2)}, u32[]{:S(2)}) %collective-permute-start) | collective-permute-done | bytes 524320 | tf_op jit(solution)/shard_map/ppermute | solution.py:290
  9.6 1.5 %collective-permute-start.1 = (f32[8,32,128]{2,1,0:T(8,128)S(1)}, f32[8,32,128]{2,1,0:T(8,128)S(1)}, u32[]{:S(2)}, u32[]{:S(2)}) collective-permute-start(f32[8,32,128]{2,1,0:T(8,128)S(1)} %get-tuple-element.80), channel_id=1, source_target_pairs={{0,32},{32,64},{64,96},{96,0},{1,33},{33,65},{65,97},{97,1},{2,34}... | collective-permute-start | bytes 393224 | tf_op jit(solution)/shard_map/ppermute | solution.py:290
  11.0 2.6 %collective-permute-start.2 = (f32[8,32,128]{2,1,0:T(8,128)S(1)}, f32[8,32,128]{2,1,0:T(8,128)S(1)}, u32[]{:S(2)}, u32[]{:S(2)}) collective-permute-start(f32[8,32,128]{2,1,0:T(8,128)S(1)} %get-tuple-element.81), channel_id=1, source_target_pairs={{0,64},{32,96},{64,0},{96,32},{1,65},{33,97},{65,1},{97,33},{2,66}... | collective-permute-start | bytes 393224 | tf_op jit(solution)/shard_map/ppermute | solution.py:290
  13.6 1.1 collective-permute-start.3
  14.7 1.1 %collective-permute-done.1.a = f32[8,32,128]{2,1,0:T(8,128)S(1)} collective-permute-done((f32[8,32,128]{2,1,0:T(8,128)S(1)}, f32[8,32,128]{2,1,0:T(8,128)S(1)}, u32[]{:S(2)}, u32[]{:S(2)}) %collective-permute-start.1) | collective-permute-done | bytes 131104 | tf_op jit(solution)/shard_map/ppermute | solution.py:290
  15.9 3.8 %collective-permute-done.2.b = f32[8,32,128]{2,1,0:T(8,128)S(1)} collective-permute-done((f32[8,32,128]{2,1,0:T(8,128)S(1)}, f32[8,32,128]{2,1,0:T(8,128)S(1)}, u32[]{:S(2)}, u32[]{:S(2)}) %collective-permute-start.2) | collective-permute-done | bytes 131104 | tf_op jit(solution)/shard_map/ppermute | solution.py:290
  20.8 2.3 %collective-permute-start.5 = (f32[8,32,128]{2,1,0:T(8,128)S(1)}, f32[8,32,128]{2,1,0:T(8,128)S(1)}, u32[]{:S(2)}, u32[]{:S(2)}) collective-permute-start(f32[8,32,128]{2,1,0:T(8,128)S(1)} %get-tuple-element.83.refs_0_), channel_id=1, source_target_pairs={{0,64},{32,96},{64,0},{96,32},{1,65},{33,97},{65,1},{97,33},{2,66}... | collective-permute-start | bytes 393224 | tf_op jit(solution)/shard_map/ppermute | solution.py:290
  23.9 2.3 %collective-permute-start.7 = (f32[8,32,128]{2,1,0:T(8,128)S(1)}, f32[8,32,128]{2,1,0:T(8,128)S(1)}, u32[]{:S(2)}, u32[]{:S(2)}) collective-permute-start(f32[8,32,128]{2,1,0:T(8,128)S(1)} %get-tuple-element.83.refs_0_), channel_id=1, source_target_pairs={{0,16},{16,0},{1,17},{17,1},{2,18},{18,2},{3,19},{19,3},{4,20},{20... | collective-permute-start | bytes 393224 | tf_op jit(solution)/shard_map/ppermute | solution.py:290
  26.2 2.2 %collective-permute-start.10 = (f32[8,32,128]{2,1,0:T(8,128)S(1)}, f32[8,32,128]{2,1,0:T(8,128)S(1)}, u32[]{:S(2)}, u32[]{:S(2)}) collective-permute-start(f32[8,32,128]{2,1,0:T(8,128)S(1)} %collective-permute-done.6.refs_3_), channel_id=1, source_target_pairs={{0,16},{16,0},{1,17},{17,1},{2,18},{18,2},{3,19},{19,3},{4,20},{20... | collective-permute-start | bytes 393224 | tf_op jit(solution)/shard_map/ppermute | solution.py:290
  28.4 1.9 %collective-permute-start.9 = (f32[8,32,128]{2,1,0:T(8,128)S(1)}, f32[8,32,128]{2,1,0:T(8,128)S(1)}, u32[]{:S(2)}, u32[]{:S(2)}) collective-permute-start(f32[8,32,128]{2,1,0:T(8,128)S(1)} %collective-permute-done.5.refs_2_), channel_id=1, source_target_pairs={{0,16},{16,0},{1,17},{17,1},{2,18},{18,2},{3,19},{19,3},{4,20},{20... | collective-permute-start | bytes 393224 | tf_op jit(solution)/shard_map/ppermute | solution.py:290
  31.7 5.4 %shard_map.80 = (f32[4,8,32,128]{3,2,1,0:T(8,128)S(1)}, f32[4,8,32,128]{3,2,1,0:T(8,128)S(1)}, f32[32,32,128]{2,1,0:T(8,128)S(1)}, f32[1,8,128]{2,1,0:T(8,128)S(1)}) custom-call(s32[256]{0:T(256)S(1)} %copy-done.2, s32[256]{0:T(256)S(1)} %copy-done.3, s32[2]{0:T(128)S(1)} %pad_add_fusion.me, bf16[64,128,256]{2,1,0:T(8,128)(2,1)S(1)} %get-tuple-element.75.plain, ...), custom_call_target="tpu_custom_call" | custom-call | flops 1000000 | bytes 1048576 | tf_op jit(solution)/shard_map/pallas_call | solution.py:30
  37.4 6.0 %collective-permute-start.15 = (f32[32,8,128]{2,1,0:T(8,128)S(1)}, f32[32,8,128]{2,1,0:T(8,128)S(1)}, u32[]{:S(2)}, u32[]{:S(2)}) collective-permute-start(f32[32,8,128]{2,1,0:T(8,128)S(1)} %get-tuple-element.94), channel_id=1, source_target_pairs={{1,0},{2,1},{3,2},{4,3},{5,4},{6,5},{7,6},{8,7},{9,8},{10,9},{11,1... | collective-permute-start | bytes 393224 | tf_op jit(solution)/shard_map/ppermute | solution.py:351
  43.4 1.3 %collective-permute-start.12 = (f32[8,32,128]{2,1,0:T(8,128)S(1)}, f32[8,32,128]{2,1,0:T(8,128)S(1)}, u32[]{:S(2)}, u32[]{:S(2)}) collective-permute-start(f32[8,32,128]{2,1,0:T(8,128)S(1)} %get-tuple-element.91), channel_id=1, source_target_pairs={{0,32},{32,64},{64,96},{96,0},{1,33},{33,65},{65,97},{97,1},{2,34}... | collective-permute-start | bytes 393224 | tf_op jit(solution)/shard_map/ppermute | solution.py:290
  44.7 2.1 %collective-permute-start.13 = (f32[8,32,128]{2,1,0:T(8,128)S(1)}, f32[8,32,128]{2,1,0:T(8,128)S(1)}, u32[]{:S(2)}, u32[]{:S(2)}) collective-permute-start(f32[8,32,128]{2,1,0:T(8,128)S(1)} %get-tuple-element.92), channel_id=1, source_target_pairs={{0,64},{32,96},{64,0},{96,32},{1,65},{33,97},{65,1},{97,33},{2,66}... | collective-permute-start | bytes 393224 | tf_op jit(solution)/shard_map/ppermute | solution.py:290
  47.4 3.7 %collective-permute-done.16.last0 = f32[32,8,128]{2,1,0:T(8,128)S(1)} collective-permute-done((f32[32,8,128]{2,1,0:T(8,128)S(1)}, f32[32,8,128]{2,1,0:T(8,128)S(1)}, u32[]{:S(2)}, u32[]{:S(2)}) %collective-permute-start.16) | collective-permute-done | bytes 131104 | tf_op jit(solution)/shard_map/ppermute | solution.py:351
  51.1 1.7 %collective-permute-done.13.b = f32[8,32,128]{2,1,0:T(8,128)S(1)} collective-permute-done((f32[8,32,128]{2,1,0:T(8,128)S(1)}, f32[8,32,128]{2,1,0:T(8,128)S(1)}, u32[]{:S(2)}, u32[]{:S(2)}) %collective-permute-start.13) | collective-permute-done | bytes 131104 | tf_op jit(solution)/shard_map/ppermute | solution.py:290
  53.5 1.9 %collective-permute-start.19 = (f32[8,32,128]{2,1,0:T(8,128)S(1)}, f32[8,32,128]{2,1,0:T(8,128)S(1)}, u32[]{:S(2)}, u32[]{:S(2)}) collective-permute-start(f32[8,32,128]{2,1,0:T(8,128)S(1)} %get-tuple-element.100.refs_0_), channel_id=1, source_target_pairs={{0,32},{32,64},{64,96},{96,0},{1,33},{33,65},{65,97},{97,1},{2,34}... | collective-permute-start | bytes 393224 | tf_op jit(solution)/shard_map/ppermute | solution.py:290
  55.4 2.0 %collective-permute-start.18 = (f32[8,32,128]{2,1,0:T(8,128)S(1)}, f32[8,32,128]{2,1,0:T(8,128)S(1)}, u32[]{:S(2)}, u32[]{:S(2)}) collective-permute-start(f32[8,32,128]{2,1,0:T(8,128)S(1)} %get-tuple-element.100.refs_0_), channel_id=1, source_target_pairs={{0,64},{32,96},{64,0},{96,32},{1,65},{33,97},{65,1},{97,33},{2,66}... | collective-permute-start | bytes 393224 | tf_op jit(solution)/shard_map/ppermute | solution.py:290
  57.8 1.6 %collective-permute-start.20 = (f32[8,32,128]{2,1,0:T(8,128)S(1)}, f32[8,32,128]{2,1,0:T(8,128)S(1)}, u32[]{:S(2)}, u32[]{:S(2)}) collective-permute-start(f32[8,32,128]{2,1,0:T(8,128)S(1)} %get-tuple-element.100.refs_0_), channel_id=1, source_target_pairs={{0,16},{16,0},{1,17},{17,1},{2,18},{18,2},{3,19},{19,3},{4,20},{20... | collective-permute-start | bytes 393224 | tf_op jit(solution)/shard_map/ppermute | solution.py:290
  59.4 1.9 %collective-permute-start.23 = (f32[8,32,128]{2,1,0:T(8,128)S(1)}, f32[8,32,128]{2,1,0:T(8,128)S(1)}, u32[]{:S(2)}, u32[]{:S(2)}) collective-permute-start(f32[8,32,128]{2,1,0:T(8,128)S(1)} %collective-permute-done.19.refs_3_), channel_id=1, source_target_pairs={{0,16},{16,0},{1,17},{17,1},{2,18},{18,2},{3,19},{19,3},{4,20},{20... | collective-permute-start | bytes 393224 | tf_op jit(solution)/shard_map/ppermute | solution.py:290
  61.3 1.7 %collective-permute-done.18.refs_2_ = f32[8,32,128]{2,1,0:T(8,128)S(1)} collective-permute-done((f32[8,32,128]{2,1,0:T(8,128)S(1)}, f32[8,32,128]{2,1,0:T(8,128)S(1)}, u32[]{:S(2)}, u32[]{:S(2)}) %collective-permute-start.18) | collective-permute-done | bytes 131104 | tf_op jit(solution)/shard_map/ppermute | solution.py:290
  63.0 1.7 %collective-permute-start.22 = (f32[8,32,128]{2,1,0:T(8,128)S(1)}, f32[8,32,128]{2,1,0:T(8,128)S(1)}, u32[]{:S(2)}, u32[]{:S(2)}) collective-permute-start(f32[8,32,128]{2,1,0:T(8,128)S(1)} %collective-permute-done.18.refs_2_), channel_id=1, source_target_pairs={{0,16},{16,0},{1,17},{17,1},{2,18},{18,2},{3,19},{19,3},{4,20},{20... | collective-permute-start | bytes 393224 | tf_op jit(solution)/shard_map/ppermute | solution.py:290
  66.0 5.5 %shard_map.83 = (f32[4,8,32,128]{3,2,1,0:T(8,128)S(1)}, f32[4,8,32,128]{3,2,1,0:T(8,128)S(1)}, f32[32,32,128]{2,1,0:T(8,128)S(1)}, f32[2,8,128]{2,1,0:T(8,128)S(...) custom-call(s32[256]{0:T(256)S(1)} %copy-done.2, s32[256]{0:T(256)S(1)} %copy-done.3, s32[2]{0:T(128)S(1)} %pad_add_fusion.me, ...), custom_call_target="tpu_custom_call" | custom-call | flops 1000000 | bytes 1048576 | tf_op jit(solution)/shard_map/pallas_call | solution.py:30
  71.8 1.7 %collective-permute-done.24.got = f32[4,8,32,128]{3,2,1,0:T(8,128)S(1)} collective-permute-done((f32[4,8,32,128]{3,2,1,0:T(8,128)S(1)}, f32[4,8,32,128]{3,2,1,0:T(8,128)S(1)}, u32[]{:S(2)}, u32[]{:S(2)}) %collective-permute-start.24) | collective-permute-done | bytes 524320 | tf_op jit(solution)/shard_map/ppermute | solution.py:290
  74.1 2.1 %collective-permute-start.26 = (f32[8,32,128]{2,1,0:T(8,128)S(1)}, f32[8,32,128]{2,1,0:T(8,128)S(1)}, u32[]{:S(2)}, u32[]{:S(2)}) collective-permute-start(f32[8,32,128]{2,1,0:T(8,128)S(1)} %get-tuple-element.106), channel_id=1, source_target_pairs={{0,64},{32,96},{64,0},{96,32},{1,65},{33,97},{65,1},{97,33},{2,66}... | collective-permute-start | bytes 393224 | tf_op jit(solution)/shard_map/ppermute | solution.py:290
  77.0 4.5 %collective-permute-start.28 = (f32[32,8,128]{2,1,0:T(8,128)S(1)}, f32[32,8,128]{2,1,0:T(8,128)S(1)}, u32[]{:S(2)}, u32[]{:S(2)}) collective-permute-start(f32[32,8,128]{2,1,0:T(8,128)S(1)} %get-tuple-element.113), channel_id=1, source_target_pairs={{1,0},{2,1},{3,2},{4,3},{5,4},{6,5},{7,6},{8,7},{9,8},{10,9},{11,1... | collective-permute-start | bytes 393224 | tf_op jit(solution)/shard_map/ppermute | solution.py:363
  82.8 1.2 %shard_map.85 = (f32[8,32,128]{2,1,0:T(8,128)S(1)}, f32[128,128]{1,0:T(8,128)S(1)}) custom-call(f32[8,32,128]{2,1,0:T(8,128)S(1)} %get-tuple-element.104.kept, f32[8,32,128]{2,1,0:T(8,128)S(1)} %collective-permute-done.25.a, f32[8,32,128]{2,1,0:T(8,128)S(1)} %collective-permute-done.26.b, f32[8,32,128]{2,1,0:T(8,128)S(1)} %collective-permute-done.27.c, ...), custom_call_target="tpu_custom_call" | custom-call | flops 1000000 | bytes 1048576 | tf_op jit(solution)/shard_map/pallas_call | solution.py:30
  84.0 4.6 %collective-permute-done.29.last = f32[32,8,128]{2,1,0:T(8,128)S(1)} collective-permute-done((f32[32,8,128]{2,1,0:T(8,128)S(1)}, f32[32,8,128]{2,1,0:T(8,128)S(1)}, u32[]{:S(2)}, u32[]{:S(2)}) %collective-permute-start.29) | collective-permute-done | bytes 131104 | tf_op jit(solution)/shard_map/ppermute | solution.py:363
  88.6 15.3 %all_to_all.20 = f32[128,1,128]{2,1,0:T(1,128)S(1)} all-to-all(f32[128,1,128]{2,1,0:T(1,128)S(1)} %bitcast.16), channel_id=1, replica_groups=mesh['tile_0'=4,'tile_1'=2,'slab_0'=4,'slab_1'=4] {'tile_0','tile_1','sl..., dimensions={0} | all-to-all | bytes 131072 | tf_op jit(solution)/shard_map/all_to_all | solution.py:308
  105.5 2.6 %shard_map.87 = (f32[32,4096]{1,0:T(8,128)}, f32[32,1024]{1,0:T(8,128)}) custom-call(s32[2]{0:T(128)S(1)} %add_convert_fusion.ends, f32[2]{0:T(128)S(1)} %get-tuple-element.126.alphas, f32[32,4096]{1,0:T(8,128)S(1)} %copy-done, f32[32,32,128]{2,1,0:T(8,128)S(1)} %get-tuple-element.101.refs_8_.grad, f32[32,32,128]{2,1,0:T(8,128)S(1)} %get-tuple-element.120.turned, ...), custom_call_target="tpu_custom_call" | custom-call | flops 1000000 | bytes 1048576 | tf_op jit(solution)/shard_map/pallas_call | solution.py:30
  (53 shorter events, 10.6 us)
Async XLA Ops:
  0.6 31.0 %copy-start.3 = (s32[256]{0:T(256)S(1)}, s32[256]{0:T(256)}, u32[]{:S(2)}) copy-start(s32[256]{0:T(256)} %strips.3) | copy-start | bytes 3076
  6.5 3.0 %collective-permute-start = (f32[4,8,32,128]{3,2,1,0:T(8,128)S(1)}, f32[4,8,32,128]{3,2,1,0:T(8,128)S(1)}, u32[]{:S(2)}, u32[]{:S(2)}) collective-permute-start(f32[4,8,32,128]{3,2,1,0:T(8,128)S(1)} %get-tuple-element.78), channel_id=1, source_target_pairs={{0,16},{16,0},{1,17},{17,1},{2,18},{18,2},{3,19},{19,3},{4,20},{20... | collective-permute-start | bytes 1572872 | tf_op jit(solution)/shard_map/ppermute | solution.py:290
  9.6 6.3 %collective-permute-start.1 = (f32[8,32,128]{2,1,0:T(8,128)S(1)}, f32[8,32,128]{2,1,0:T(8,128)S(1)}, u32[]{:S(2)}, u32[]{:S(2)}) collective-permute-start(f32[8,32,128]{2,1,0:T(8,128)S(1)} %get-tuple-element.80), channel_id=1, source_target_pairs={{0,32},{32,64},{64,96},{96,0},{1,33},{33,65},{65,97},{97,1},{2,34}... | collective-permute-start | bytes 393224 | tf_op jit(solution)/shard_map/ppermute | solution.py:290
  11.0 8.6 %collective-permute-start.2 = (f32[8,32,128]{2,1,0:T(8,128)S(1)}, f32[8,32,128]{2,1,0:T(8,128)S(1)}, u32[]{:S(2)}, u32[]{:S(2)}) collective-permute-start(f32[8,32,128]{2,1,0:T(8,128)S(1)} %get-tuple-element.81), channel_id=1, source_target_pairs={{0,64},{32,96},{64,0},{96,32},{1,65},{33,97},{65,1},{97,33},{2,66}... | collective-permute-start | bytes 393224 | tf_op jit(solution)/shard_map/ppermute | solution.py:290
  13.6 6.0 %collective-permute-start.3 = (f32[8,32,128]{2,1,0:T(8,128)S(1)}, f32[8,32,128]{2,1,0:T(8,128)S(1)}, u32[]{:S(2)}, u32[]{:S(2)}) collective-permute-start(f32[8,32,128]{2,1,0:T(8,128)S(1)} %get-tuple-element.82), channel_id=1, source_target_pairs={{0,96},{32,0},{64,32},{96,64},{1,97},{33,1},{65,33},{97,65},{2,98}... | collective-permute-start | bytes 393224 | tf_op jit(solution)/shard_map/ppermute | solution.py:290
  19.7 6.5 %collective-permute-start.6 = (f32[8,32,128]{2,1,0:T(8,128)S(1)}, f32[8,32,128]{2,1,0:T(8,128)S(1)}, u32[]{:S(2)}, u32[]{:S(2)}) collective-permute-start(f32[8,32,128]{2,1,0:T(8,128)S(1)} %get-tuple-element.83.refs_0_), channel_id=1, source_target_pairs={{0,32},{32,64},{64,96},{96,0},{1,33},{33,65},{65,97},{97,1},{2,34}... | collective-permute-start | bytes 393224 | tf_op jit(solution)/shard_map/ppermute | solution.py:290
  20.8 7.6 %collective-permute-start.5 = (f32[8,32,128]{2,1,0:T(8,128)S(1)}, f32[8,32,128]{2,1,0:T(8,128)S(1)}, u32[]{:S(2)}, u32[]{:S(2)}) collective-permute-start(f32[8,32,128]{2,1,0:T(8,128)S(1)} %get-tuple-element.83.refs_0_), channel_id=1, source_target_pairs={{0,64},{32,96},{64,0},{96,32},{1,65},{33,97},{65,1},{97,33},{2,66}... | collective-permute-start | bytes 393224 | tf_op jit(solution)/shard_map/ppermute | solution.py:290
  23.1 7.3 %collective-permute-start.4 = (f32[8,32,128]{2,1,0:T(8,128)S(1)}, f32[8,32,128]{2,1,0:T(8,128)S(1)}, u32[]{:S(2)}, u32[]{:S(2)}) collective-permute-start(f32[8,32,128]{2,1,0:T(8,128)S(1)} %get-tuple-element.83.refs_0_), channel_id=1, source_target_pairs={{0,96},{32,0},{64,32},{96,64},{1,97},{33,1},{65,33},{97,65},{2,98}... | collective-permute-start | bytes 393224 | tf_op jit(solution)/shard_map/ppermute | solution.py:290
  23.9 6.4 %collective-permute-start.7 = (f32[8,32,128]{2,1,0:T(8,128)S(1)}, f32[8,32,128]{2,1,0:T(8,128)S(1)}, u32[]{:S(2)}, u32[]{:S(2)}) collective-permute-start(f32[8,32,128]{2,1,0:T(8,128)S(1)} %get-tuple-element.83.refs_0_), channel_id=1, source_target_pairs={{0,16},{16,0},{1,17},{17,1},{2,18},{18,2},{3,19},{19,3},{4,20},{20... | collective-permute-start | bytes 393224 | tf_op jit(solution)/shard_map/ppermute | solution.py:290
  26.2 4.1 %collective-permute-start.10 = (f32[8,32,128]{2,1,0:T(8,128)S(1)}, f32[8,32,128]{2,1,0:T(8,128)S(1)}, u32[]{:S(2)}, u32[]{:S(2)}) collective-permute-start(f32[8,32,128]{2,1,0:T(8,128)S(1)} %collective-permute-done.6.refs_3_), channel_id=1, source_target_pairs={{0,16},{16,0},{1,17},{17,1},{2,18},{18,2},{3,19},{19,3},{4,20},{20... | collective-permute-start | bytes 393224 | tf_op jit(solution)/shard_map/ppermute | solution.py:290
  28.4 2.9 %collective-permute-start.9 = (f32[8,32,128]{2,1,0:T(8,128)S(1)}, f32[8,32,128]{2,1,0:T(8,128)S(1)}, u32[]{:S(2)}, u32[]{:S(2)}) collective-permute-start(f32[8,32,128]{2,1,0:T(8,128)S(1)} %collective-permute-done.5.refs_2_), channel_id=1, source_target_pairs={{0,16},{16,0},{1,17},{17,1},{2,18},{18,2},{3,19},{19,3},{4,20},{20... | collective-permute-start | bytes 393224 | tf_op jit(solution)/shard_map/ppermute | solution.py:290
  30.3 1.3 %collective-permute-start.8 = (f32[8,32,128]{2,1,0:T(8,128)S(1)}, f32[8,32,128]{2,1,0:T(8,128)S(1)}, u32[]{:S(2)}, u32[]{:S(2)}) collective-permute-start(f32[8,32,128]{2,1,0:T(8,128)S(1)} %collective-permute-done.4.refs_1_), channel_id=1, source_target_pairs={{0,16},{16,0},{1,17},{17,1},{2,18},{18,2},{3,19},{19,3},{4,20},{20... | collective-permute-start | bytes 393224 | tf_op jit(solution)/shard_map/ppermute | solution.py:290
  37.1 6.2 %collective-permute-start.11 = (f32[4,8,32,128]{3,2,1,0:T(8,128)S(1)}, f32[4,8,32,128]{3,2,1,0:T(8,128)S(1)}, u32[]{:S(2)}, u32[]{:S(2)}) collective-permute-start(f32[4,8,32,128]{3,2,1,0:T(8,128)S(1)} %get-tuple-element.89), channel_id=1, source_target_pairs={{0,16},{16,0},{1,17},{17,1},{2,18},{18,2},{3,19},{19,3},{4,20},{20... | collective-permute-start | bytes 1572872 | tf_op jit(solution)/shard_map/ppermute | solution.py:290
  37.4 10.1 %collective-permute-start.15 = (f32[32,8,128]{2,1,0:T(8,128)S(1)}, f32[32,8,128]{2,1,0:T(8,128)S(1)}, u32[]{:S(2)}, u32[]{:S(2)}) collective-permute-start(f32[32,8,128]{2,1,0:T(8,128)S(1)} %get-tuple-element.94), channel_id=1, source_target_pairs={{1,0},{2,1},{3,2},{4,3},{5,4},{6,5},{7,6},{8,7},{9,8},{10,9},{11,1... | collective-permute-start | bytes 393224 | tf_op jit(solution)/shard_map/ppermute | solution.py:351
  43.3 7.8 %collective-permute-start.16 = (f32[32,8,128]{2,1,0:T(8,128)S(1)}, f32[32,8,128]{2,1,0:T(8,128)S(1)}, u32[]{:S(2)}, u32[]{:S(2)}) collective-permute-start(f32[32,8,128]{2,1,0:T(8,128)S(1)} %get-tuple-element.95), channel_id=1, source_target_pairs={{0,1},{1,2},{2,3},{3,4},{4,5},{5,6},{6,7},{7,8},{8,9},{9,10},{10,1... | collective-permute-start | bytes 393224 | tf_op jit(solution)/shard_map/ppermute | solution.py:351
  43.4 7.7 %collective-permute-start.12 = (f32[8,32,128]{2,1,0:T(8,128)S(1)}, f32[8,32,128]{2,1,0:T(8,128)S(1)}, u32[]{:S(2)}, u32[]{:S(2)}) collective-permute-start(f32[8,32,128]{2,1,0:T(8,128)S(1)} %get-tuple-element.91), channel_id=1, source_target_pairs={{0,32},{32,64},{64,96},{96,0},{1,33},{33,65},{65,97},{97,1},{2,34}... | collective-permute-start | bytes 393224 | tf_op jit(solution)/shard_map/ppermute | solution.py:290
  44.7 8.1 %collective-permute-start.13 = (f32[8,32,128]{2,1,0:T(8,128)S(1)}, f32[8,32,128]{2,1,0:T(8,128)S(1)}, u32[]{:S(2)}, u32[]{:S(2)}) collective-permute-start(f32[8,32,128]{2,1,0:T(8,128)S(1)} %get-tuple-element.92), channel_id=1, source_target_pairs={{0,64},{32,96},{64,0},{96,32},{1,65},{33,97},{65,1},{97,33},{2,66}... | collective-permute-start | bytes 393224 | tf_op jit(solution)/shard_map/ppermute | solution.py:290
  46.8 6.0 %collective-permute-start.14 = (f32[8,32,128]{2,1,0:T(8,128)S(1)}, f32[8,32,128]{2,1,0:T(8,128)S(1)}, u32[]{:S(2)}, u32[]{:S(2)}) collective-permute-start(f32[8,32,128]{2,1,0:T(8,128)S(1)} %get-tuple-element.93), channel_id=1, source_target_pairs={{0,96},{32,0},{64,32},{96,64},{1,97},{33,1},{65,33},{97,65},{2,98}... | collective-permute-start | bytes 393224 | tf_op jit(solution)/shard_map/ppermute | solution.py:290
  53.5 5.9 %collective-permute-start.19 = (f32[8,32,128]{2,1,0:T(8,128)S(1)}, f32[8,32,128]{2,1,0:T(8,128)S(1)}, u32[]{:S(2)}, u32[]{:S(2)}) collective-permute-start(f32[8,32,128]{2,1,0:T(8,128)S(1)} %get-tuple-element.100.refs_0_), channel_id=1, source_target_pairs={{0,32},{32,64},{64,96},{96,0},{1,33},{33,65},{65,97},{97,1},{2,34}... | collective-permute-start | bytes 393224 | tf_op jit(solution)/shard_map/ppermute | solution.py:290
  55.4 7.6 %collective-permute-start.18 = (f32[8,32,128]{2,1,0:T(8,128)S(1)}, f32[8,32,128]{2,1,0:T(8,128)S(1)}, u32[]{:S(2)}, u32[]{:S(2)}) collective-permute-start(f32[8,32,128]{2,1,0:T(8,128)S(1)} %get-tuple-element.100.refs_0_), channel_id=1, source_target_pairs={{0,64},{32,96},{64,0},{96,32},{1,65},{33,97},{65,1},{97,33},{2,66}... | collective-permute-start | bytes 393224 | tf_op jit(solution)/shard_map/ppermute | solution.py:290
  57.4 7.3 %collective-permute-start.17 = (f32[8,32,128]{2,1,0:T(8,128)S(1)}, f32[8,32,128]{2,1,0:T(8,128)S(1)}, u32[]{:S(2)}, u32[]{:S(2)}) collective-permute-start(f32[8,32,128]{2,1,0:T(8,128)S(1)} %get-tuple-element.100.refs_0_), channel_id=1, source_target_pairs={{0,96},{32,0},{64,32},{96,64},{1,97},{33,1},{65,33},{97,65},{2,98}... | collective-permute-start | bytes 393224 | tf_op jit(solution)/shard_map/ppermute | solution.py:290
  57.8 6.9 %collective-permute-start.20 = (f32[8,32,128]{2,1,0:T(8,128)S(1)}, f32[8,32,128]{2,1,0:T(8,128)S(1)}, u32[]{:S(2)}, u32[]{:S(2)}) collective-permute-start(f32[8,32,128]{2,1,0:T(8,128)S(1)} %get-tuple-element.100.refs_0_), channel_id=1, source_target_pairs={{0,16},{16,0},{1,17},{17,1},{2,18},{18,2},{3,19},{19,3},{4,20},{20... | collective-permute-start | bytes 393224 | tf_op jit(solution)/shard_map/ppermute | solution.py:290
  59.4 5.2 %collective-permute-start.23 = (f32[8,32,128]{2,1,0:T(8,128)S(1)}, f32[8,32,128]{2,1,0:T(8,128)S(1)}, u32[]{:S(2)}, u32[]{:S(2)}) collective-permute-start(f32[8,32,128]{2,1,0:T(8,128)S(1)} %collective-permute-done.19.refs_3_), channel_id=1, source_target_pairs={{0,16},{16,0},{1,17},{17,1},{2,18},{18,2},{3,19},{19,3},{4,20},{20... | collective-permute-start | bytes 393224 | tf_op jit(solution)/shard_map/ppermute | solution.py:290
  63.0 2.6 %collective-permute-start.22 = (f32[8,32,128]{2,1,0:T(8,128)S(1)}, f32[8,32,128]{2,1,0:T(8,128)S(1)}, u32[]{:S(2)}, u32[]{:S(2)}) collective-permute-start(f32[8,32,128]{2,1,0:T(8,128)S(1)} %collective-permute-done.18.refs_2_), channel_id=1, source_target_pairs={{0,16},{16,0},{1,17},{17,1},{2,18},{18,2},{3,19},{19,3},{4,20},{20... | collective-permute-start | bytes 393224 | tf_op jit(solution)/shard_map/ppermute | solution.py:290
  64.7 1.3 %collective-permute-start.21 = (f32[8,32,128]{2,1,0:T(8,128)S(1)}, f32[8,32,128]{2,1,0:T(8,128)S(1)}, u32[]{:S(2)}, u32[]{:S(2)}) collective-permute-start(f32[8,32,128]{2,1,0:T(8,128)S(1)} %collective-permute-done.17.refs_1_), channel_id=1, source_target_pairs={{0,16},{16,0},{1,17},{17,1},{2,18},{18,2},{3,19},{19,3},{4,20},{20... | collective-permute-start | bytes 393224 | tf_op jit(solution)/shard_map/ppermute | solution.py:290
  71.5 34.0 %copy-start = (f32[32,4096]{1,0:T(8,128)S(1)}, f32[32,4096]{1,0:T(8,128)}, u32[]{:S(2)}) copy-start(f32[32,4096]{1,0:T(8,128)} %volume.1) | copy-start | bytes 1572868
  71.5 2.0 %collective-permute-start.24 = (f32[4,8,32,128]{3,2,1,0:T(8,128)S(1)}, f32[4,8,32,128]{3,2,1,0:T(8,128)S(1)}, u32[]{:S(2)}, u32[]{:S(2)}) collective-permute-start(f32[4,8,32,128]{3,2,1,0:T(8,128)S(1)} %get-tuple-element.103), channel_id=1, source_target_pairs={{0,16},{16,0},{1,17},{17,1},{2,18},{18,2},{3,19},{19,3},{4,20},{20... | collective-permute-start | bytes 1572872 | tf_op jit(solution)/shard_map/ppermute | solution.py:290
  73.6 8.0 %collective-permute-start.25 = (f32[8,32,128]{2,1,0:T(8,128)S(1)}, f32[8,32,128]{2,1,0:T(8,128)S(1)}, u32[]{:S(2)}, u32[]{:S(2)}) collective-permute-start(f32[8,32,128]{2,1,0:T(8,128)S(1)} %get-tuple-element.105), channel_id=1, source_target_pairs={{0,32},{32,64},{64,96},{96,0},{1,33},{33,65},{65,97},{97,1},{2,34}... | collective-permute-start | bytes 393224 | tf_op jit(solution)/shard_map/ppermute | solution.py:290
  74.1 8.2 %collective-permute-start.26 = (f32[8,32,128]{2,1,0:T(8,128)S(1)}, f32[8,32,128]{2,1,0:T(8,128)S(1)}, u32[]{:S(2)}, u32[]{:S(2)}) collective-permute-start(f32[8,32,128]{2,1,0:T(8,128)S(1)} %get-tuple-element.106), channel_id=1, source_target_pairs={{0,64},{32,96},{64,0},{96,32},{1,65},{33,97},{65,1},{97,33},{2,66}... | collective-permute-start | bytes 393224 | tf_op jit(solution)/shard_map/ppermute | solution.py:290
  76.2 6.6 %collective-permute-start.27 = (f32[8,32,128]{2,1,0:T(8,128)S(1)}, f32[8,32,128]{2,1,0:T(8,128)S(1)}, u32[]{:S(2)}, u32[]{:S(2)}) collective-permute-start(f32[8,32,128]{2,1,0:T(8,128)S(1)} %get-tuple-element.107), channel_id=1, source_target_pairs={{0,96},{32,0},{64,32},{96,64},{1,97},{33,1},{65,33},{97,65},{2,98}... | collective-permute-start | bytes 393224 | tf_op jit(solution)/shard_map/ppermute | solution.py:290
  77.0 7.0 %collective-permute-start.28 = (f32[32,8,128]{2,1,0:T(8,128)S(1)}, f32[32,8,128]{2,1,0:T(8,128)S(1)}, u32[]{:S(2)}, u32[]{:S(2)}) collective-permute-start(f32[32,8,128]{2,1,0:T(8,128)S(1)} %get-tuple-element.113), channel_id=1, source_target_pairs={{1,0},{2,1},{3,2},{4,3},{5,4},{6,5},{7,6},{8,7},{9,8},{10,9},{11,1... | collective-permute-start | bytes 393224 | tf_op jit(solution)/shard_map/ppermute | solution.py:363
  81.5 7.1 %collective-permute-start.29 = (f32[32,8,128]{2,1,0:T(8,128)S(1)}, f32[32,8,128]{2,1,0:T(8,128)S(1)}, u32[]{:S(2)}, u32[]{:S(2)}) collective-permute-start(f32[32,8,128]{2,1,0:T(8,128)S(1)} %get-tuple-element.114), channel_id=1, source_target_pairs={{0,1},{1,2},{2,3},{3,4},{4,5},{5,6},{6,7},{7,8},{8,9},{9,10},{10,1... | collective-permute-start | bytes 393224 | tf_op jit(solution)/shard_map/ppermute | solution.py:363
  (3 other events, 69.1 us)
where the time goes:
time: 108 us
  starting transfers between devices  45.2 us (42%)
  waiting for transfers between devices  23.9 us (22%)
  Pallas kernels  22.1 us (20%)
  blocking collectives  15.3 us (14%)
  between operations  1.43 us (1%)
    ppermute x26, starting transfers between devices, shift(): return lax.ppermute(value, axis, [(i, (i + by) % n) for i in range(n)])  34.7 us
    pallas_call x10, Pallas kernels, call(): pl.pallas_call(kernel, out_shape=[s if hasattr(s, 'dtype') else jax.Shape...  21.3 us
    ppermute x26, waiting for transfers between devices, shift(): return lax.ppermute(value, axis, [(i, (i + by) % n) for i in range(n)])  15.5 us
    all_to_all x1, blocking collectives, over_all(): return lax.all_to_all(rows, TILE + SLAB, 0, 0, tiled=True)  15.3 us
    ppermute x1, starting transfers between devices, shards(): lax.ppermute(first0, SLAB, down)  5.96 us
    ppermute x1, waiting for transfers between devices, shards(): lax.ppermute(last, SLAB, up)  4.63 us
    ppermute x1, starting transfers between devices, shards(): lax.ppermute(first, SLAB, down)  4.53 us
    ppermute x1, waiting for transfers between devices, shards(): lax.ppermute(last0, SLAB, up)  3.68 us
  transfers between devices with their start and end apart: 30, of which 14 were waited for; matrix products, arithmetic and copies ran while one was open for 0% of the time, Pallas kernels for 1%

commit v1 on v0

--- a/solution.py
+++ b/solution.py
@@ -109,8 +109,13 @@
     theirs[...] = rays[32:].reshape(theirs.shape)
 
 
+def in_pairs(me, first, last):
+    even = me[2] == 0
+    return jnp.where(even, last, first), jnp.where(even, first, last)
+
+
 def first_kernel(pixels_hbm, strips_hbm, me, foot_hbm, volume_hbm, *refs):
-    mine, theirs, first, last, plain, turned, foot, volume, high, low, rays, pixels, strips, sem, foot_sem = refs
+    mine, theirs, ahead, behind, plain, turned, foot, volume, high, low, rays, pixels, strips, sem, foot_sem = refs
     spots = (pixels, strips, me)
     per = foot.shape[0] // CHUNKS
 
@@ -135,7 +140,7 @@
     for p in range(high.shape[0]):
         cols = slice(128 * p, 128 * p + 128)
         high[p], low[p] = halves(volume[:, cols])
-        first[p], last[p] = volume[0:8, cols], volume[24:32, cols]
+        ahead[p], behind[p] = in_pairs(me, volume[0:8, cols], volume[24:32, cols])
 
     def trip(t, carry):
         chunk(t).wait()
@@ -174,14 +179,15 @@
 
 def third_kernel(pixels, strips, me, plain, turned, *refs):
     pieces, grad = refs[:8], refs[8]
-    mine, theirs, field, sums, first, last, high, low, rays = refs[9:]
+    mine, theirs, field, sums, ahead, behind, high, low, rays = refs[9:]
     there_and_back((pixels, strips, me), plain, turned, pieces, mine, theirs, field, high, low, rays)
     sums[0] = folded(grad[...] * field[...])
     sums[1] = folded(field[...] * field[...])
     row = lax.broadcasted_iota(jnp.int32, (8, 128), 0)
     for p in range(field.shape[0]):
-        first[p] = jnp.where(row < 3, grad[p, 0:8], pltpu.roll(field[p, 0:8], 3, 0))
-        last[p] = jnp.where(row > 4, grad[p, 24:32], pltpu.roll(field[p, 24:32], 5, 0))
+        first = jnp.where(row < 3, grad[p, 0:8], pltpu.roll(field[p, 0:8], 3, 0))
+        last = jnp.where(row > 4, grad[p, 24:32], pltpu.roll(field[p, 24:32], 5, 0))
+        ahead[p], behind[p] = in_pairs(me, first, last)
 
 
 def add_kernel(mine, got, kept, s1, s2, s3):
@@ -199,12 +205,14 @@
     sent[...] = tile_cols(weights) * value
 
 
-def middle_kernel(kept, a, b, c, weights, projected, sent, sums):
+def resend_kernel(kept, a, b, c, weights, sent):
+    sent[...] = tile_cols(weights) * (kept[...] + a[...] + b[...] + c[...])
+
+
+def middle_kernel(kept, a, b, c, sent, projected, sums):
     value = kept[...] + a[...] + b[...] + c[...]
-    weighted = tile_cols(weights) * value
     projected[...] = value
-    sent[...] = weighted
-    sums[0] = folded(weighted * value)
+    sums[0] = folded(sent[...] * value)
 
 
 def in_lanes(sums, shape):
@@ -232,7 +240,7 @@
     return jnp.sum(value)
 
 
-def judge_kernel(rows, alphas, again):
+def judge_kernel(rows, alphas):
     norm0, curve0, cross_g, square_g, cross_p, square_p = totals(rows, 6)
     alpha = norm0 / curve0
     norm1 = norm0 - 2.0 * alpha * cross_g + alpha * alpha * square_g
@@ -242,7 +250,7 @@
         sound = sound & (square > 1e-25) & (square < 1e37)
     alphas[0] = scalar(alpha)
     alphas[1] = scalar(norm1 / curve1)
-    again[0] = jnp.where(scalar(jnp.where(sound, F32(0.0), F32(1.0))) > 0.5, 1, 0)
+    alphas[2] = scalar(jnp.where(sound, F32(0.0), F32(1.0)))
 
 
 def again_kernel(alphas, weights, p0, q0, grad, turned, rows):
@@ -255,9 +263,10 @@
     norm1, curve1 = totals(rows, 2)
     out[0] = alphas[0]
     out[1] = scalar(norm1 / curve1)
-
-
-def smooth_kernel(ends, alphas, volume, grad, turned, first0, last0, first, last, residual, p0, q0, smoothed, left_over):
+    out[2] = F32(0.0)
+
+
+def smooth_kernel(ends, alphas, volume, grad, turned, ahead0, behind0, ahead, behind, residual, p0, q0, smoothed, left_over):
     alpha0, alpha1 = alphas[0], alphas[1]
     rest = residual[...] - alpha0 * p0[...] - alpha1 * (p0[...] - alpha0 * q0[...])
     for t in range(rest.shape[0]):
@@ -265,17 +274,23 @@
 
     def stepped(x, g, h):
         return x - alpha0 * g - alpha1 * (g - alpha0 * h)
+
+    def both_sides(behind, ahead):
+        even = ends[2] == 1
+        return jnp.where(even, behind, ahead), jnp.where(even, ahead, behind)
 
     row = lax.broadcasted_iota(jnp.int32, (48, 128), 0)
     open_link = ~(((row == 7) & (ends[0] == 1)) | ((row == 39) & (ends[1] == 1)))
     link = jnp.where(open_link, F32(1.0), F32(0.0))
     for p in range(grad.shape[0]):
         cols = slice(128 * p, 128 * p + 128)
+        last0, first0 = both_sides(behind0[p], ahead0[p])
+        last, first = both_sides(behind[p], ahead[p])
         ext = jnp.concatenate(
             [
-                stepped(last0[p], last[p], pltpu.roll(last[p], 3, 0)),
+                stepped(last0, last, pltpu.roll(last, 3, 0)),
                 stepped(volume[:, cols], grad[p], turned[p]),
-                stepped(first0[p], first[p], pltpu.roll(first[p], 5, 0)),
+                stepped(first0, first, pltpu.roll(first, 5, 0)),
             ],
             axis=0,
         )
@@ -309,13 +324,13 @@
 
 
 def shards(volume, measured, weights, footprints, foot_pixel, foot_strip):
-    me = jnp.stack([lax.axis_index("tile_0"), lax.axis_index("tile_1")])
-    spots = [foot_pixel, foot_strip, me]
     slabs = lax.axis_size(SLAB)
     place_in = lax.axis_index(SLAB)
-    ends = jnp.stack([place_in == 0, place_in == slabs - 1]).astype(jnp.int32)
-    up = [(i, (i + 1) % slabs) for i in range(slabs)]
-    down = [(j, i) for i, j in up]
+    me = jnp.stack([lax.axis_index("tile_0"), lax.axis_index("tile_1"), place_in & 1])
+    spots = [foot_pixel, foot_strip, me]
+    ends = jnp.stack([place_in == 0, place_in == slabs - 1, place_in % 2 == 0]).astype(jnp.int32)
+    evens = [(i, i ^ 1) for i in range(slabs)]
+    odds = [(i, min(max(((i + 1) ^ 1) - 1, 0), slabs - 1)) for i in range(slabs)]
 
     field, tile = (32, 32, 128), (1, 8, 128)
     scratch = [pltpu.VMEM(field, BF16), pltpu.VMEM(field, BF16), pltpu.VMEM((64, 32, 128), F32)]
@@ -331,7 +346,7 @@
     ]
     split = jax.ShapeDtypeStruct((64, 128, 256), BF16)
     half, edge = (4,) + RAY, (32, 8, 128)
-    mine, theirs, first0, last0, plain, turned = call(
+    mine, theirs, ahead0, behind0, plain, turned = call(
         first_kernel,
         [half, half, edge, edge, split, split],
         [*in_place[:2], me, *in_place[2:]],
@@ -346,13 +361,14 @@
     mine, theirs, grad, norm0 = call(
         second_kernel, [half, half, field, tile], [*spots, plain, turned, *to_everyone(sent)], scratch, 3
     )
-    mine, theirs, first0, last0 = lax.optimization_barrier((mine, theirs, first0, last0))
+    mine, theirs, ahead0, behind0 = lax.optimization_barrier((mine, theirs, ahead0, behind0))
     parts = summed_by_owner(mine, theirs)
-    first0, last0 = lax.ppermute(first0, SLAB, down), lax.ppermute(last0, SLAB, up)
-    parts, first0, last0 = lax.optimization_barrier((parts, first0, last0))
-    p0, sent, curve0 = call(middle_kernel, [RAY, RAY, tile], [*parts, weights])
-
-    mine, theirs, back, crossed, first, last = call(
+    ahead0, behind0 = lax.ppermute(ahead0, SLAB, evens), lax.ppermute(behind0, SLAB, odds)
+    parts, ahead0, behind0 = lax.optimization_barrier((parts, ahead0, behind0))
+    sent = call(resend_kernel, [RAY], [*parts, weights])[0]
+    p0, curve0 = call(middle_kernel, [RAY, tile], [*parts, sent])
+
+    mine, theirs, back, crossed, ahead, behind = call(
         third_kernel,
         [half, half, field, (2, 8, 128), edge, edge],
         [*spots, plain, turned, *to_everyone(sent), grad],
@@ -360,18 +376,18 @@
         3,
     )
     parts = summed_by_owner(mine, theirs)
-    first, last = lax.ppermute(first, SLAB, down), lax.ppermute(last, SLAB, up)
+    ahead, behind = lax.ppermute(ahead, SLAB, evens), lax.ppermute(behind, SLAB, odds)
     everyone = slabs * lax.axis_size(TILE)
     q0, rows = call(
         end_kernel, [RAY, (everyone, 128)], [*parts, weights, p0, norm0, curve0, crossed]
     )
-    rows, first, last, ends = lax.optimization_barrier((rows, first, last, ends))
+    rows, ahead, behind, ends = lax.optimization_barrier((rows, ahead, behind, ends))
     rows = over_all(rows)
-    alphas, again = pl.pallas_call(
+    alphas = pl.pallas_call(
         judge_kernel,
-        out_shape=[jax.ShapeDtypeStruct((2,), F32), jax.ShapeDtypeStruct((1,), jnp.int32)],
+        out_shape=jax.ShapeDtypeStruct((3,), F32),
         in_specs=[VM],
-        out_specs=[SM, SM],
+        out_specs=SM,
         compiler_params=pltpu.CompilerParams(vmem_limit_bytes=8 << 20),
     )(rows)
 
@@ -379,17 +395,17 @@
         rows = call(again_kernel, [(everyone, 128)], [alphas, weights, p0, q0, grad, back], (), 1)[0]
         return pl.pallas_call(
             ratio_kernel,
-            out_shape=jax.ShapeDtypeStruct((2,), F32),
+            out_shape=jax.ShapeDtypeStruct((3,), F32),
             in_specs=[SM, VM],
             out_specs=SM,
             compiler_params=pltpu.CompilerParams(vmem_limit_bytes=8 << 20),
         )(alphas, over_all(rows))
 
-    alphas = lax.cond(again[0] == 1, summed_again, lambda known: known, alphas)
+    alphas = lax.cond(alphas[2] > 0.5, summed_again, lambda known: known, alphas)
     return call(
         smooth_kernel,
         [volume.shape, measured.shape],
-        [ends, alphas, volume, grad, back, first0, last0, first, last, residual, p0, q0],
+        [ends, alphas, volume, grad, back, ahead0, behind0, ahead, behind, residual, p0, q0],
         (),
         2,
     )

time: 108 us -> 108 us (level)
  blocking collectives: 15.3 us -> 23.1 us
  starting transfers between devices: 45.2 us -> 40.3 us
  waiting for transfers between devices: 23.9 us -> 19.9 us
    ppermute x4, waiting for transfers between devices: 8.32 us -> 0.01 us  [the longest x1 0.01 us: shards(): lax.ppermute(behind, SLAB, odds)]
    all_to_all x1, blocking collectives: 15.3 us -> 23.1 us  [over_all(): return lax.all_to_all(rows, TILE + SLAB, 0, 0, tiled=True)]
    ppermute x4, starting transfers between devices: 10.5 us -> 5.61 us  [the longest x1 3.09 us: shards(): lax.ppermute(ahead, SLAB, evens)]
    ppermute x26, waiting for transfers between devices: 15.5 us -> 19.9 us  [shift(): return lax.ppermute(value, axis, [(i, (i + by) % n) for i in range(n)])]
    pallas_call x10 -> x11, Pallas kernels: 21.3 us -> 21.4 us  [call(): pl.pallas_call(kernel, out_shape=[s if hasattr(s, 'dtype') else jax.Shape...]
  transfers between devices with their start and end apart: 30 -> 30, of which waited for: 14 -> 13; matrix products, arithmetic and copies ran while one was open for 0% -> 0% of each run, Pallas kernels for 1% -> 1%
where the time goes in v1:
time: 108 us
  starting transfers between devices  40.3 us (37%)
  blocking collectives  23.1 us (21%)
  Pallas kernels  22.2 us (21%)
  waiting for transfers between devices  19.9 us (18%)
  between operations  1.5 us (1%)
    ppermute x26, starting transfers between devices, shift(): return lax.ppermute(value, axis, [(i, (i + by) % n) for i in range(n)])  34.7 us
    all_to_all x1, blocking collectives, over_all(): return lax.all_to_all(rows, TILE + SLAB, 0, 0, tiled=True)  23.1 us
    pallas_call x11, Pallas kernels, call(): pl.pallas_call(kernel, out_shape=[s if hasattr(s, 'dtype') else jax.Shape...  21.4 us
    ppermute x26, waiting for transfers between devices, shift(): return lax.ppermute(value, axis, [(i, (i + by) % n) for i in range(n)])  19.9 us
    ppermute x1, starting transfers between devices, shards(): lax.ppermute(ahead, SLAB, evens)  3.09 us
  transfers between devices with their start and end apart: 30, of which 13 were waited for; matrix products, arithmetic and copies ran while one was open for 0% of the time, Pallas kernels for 1%

profile of v1, /device:TPU:1, one launch (start us, length us, event | category | flops | bytes accessed | tf_op | source)
XLA Modules:
  0.0 107.8 jit_solution(12772888268615745700)
XLA Ops:
  0.8 5.7 %shard_map.77 = (f32[4,8,32,128]{3,2,1,0:T(8,128)S(1)}, f32[4,8,32,128]{3,2,1,0:T(8,128)S(1)}, f32[32,8,128]{2,1,0:T(8,128)S(1)}, f32[32,8,128]{2,1,0:T(8,128)S(...) custom-call(s32[256]{0:T(256)} %pixels.3, s32[256]{0:T(256)} %strips.3, s32[3]{0:T(128)S(1)} %pad_add_fusion.me, ...), custom_call_target="tpu_custom_call" | custom-call | flops 1000000 | bytes 1048576 | tf_op jit(solution)/shard_map/pallas_call | solution.py:30
  6.5 1.5 %collective-permute-start = (f32[4,8,32,128]{3,2,1,0:T(8,128)S(1)}, f32[4,8,32,128]{3,2,1,0:T(8,128)S(1)}, u32[]{:S(2)}, u32[]{:S(2)}) collective-permute-start(f32[4,8,32,128]{3,2,1,0:T(8,128)S(1)} %get-tuple-element.75), channel_id=1, source_target_pairs={{0,16},{16,0},{1,17},{17,1},{2,18},{18,2},{3,19},{19,3},{4,20},{20... | collective-permute-start | bytes 1572872 | tf_op jit(solution)/shard_map/ppermute | solution.py:305
  8.0 1.5 %collective-permute-done.got = f32[4,8,32,128]{3,2,1,0:T(8,128)S(1)} collective-permute-done((f32[4,8,32,128]{3,2,1,0:T(8,128)S(1)}, f32[4,8,32,128]{3,2,1,0:T(8,128)S(1)}, u32[]{:S(2)}, u32[]{:S(2)}) %collective-permute-start) | collective-permute-done | bytes 524320 | tf_op jit(solution)/shard_map/ppermute | solution.py:305
  9.6 1.5 %collective-permute-start.1 = (f32[8,32,128]{2,1,0:T(8,128)S(1)}, f32[8,32,128]{2,1,0:T(8,128)S(1)}, u32[]{:S(2)}, u32[]{:S(2)}) collective-permute-start(f32[8,32,128]{2,1,0:T(8,128)S(1)} %get-tuple-element.77), channel_id=1, source_target_pairs={{0,32},{32,64},{64,96},{96,0},{1,33},{33,65},{65,97},{97,1},{2,34}... | collective-permute-start | bytes 393224 | tf_op jit(solution)/shard_map/ppermute | solution.py:305
  11.0 2.6 %collective-permute-start.2 = (f32[8,32,128]{2,1,0:T(8,128)S(1)}, f32[8,32,128]{2,1,0:T(8,128)S(1)}, u32[]{:S(2)}, u32[]{:S(2)}) collective-permute-start(f32[8,32,128]{2,1,0:T(8,128)S(1)} %get-tuple-element.78), channel_id=1, source_target_pairs={{0,64},{32,96},{64,0},{96,32},{1,65},{33,97},{65,1},{97,33},{2,66}... | collective-permute-start | bytes 393224 | tf_op jit(solution)/shard_map/ppermute | solution.py:305
  14.7 1.1 %collective-permute-done.1.a = f32[8,32,128]{2,1,0:T(8,128)S(1)} collective-permute-done((f32[8,32,128]{2,1,0:T(8,128)S(1)}, f32[8,32,128]{2,1,0:T(8,128)S(1)}, u32[]{:S(2)}, u32[]{:S(2)}) %collective-permute-start.1) | collective-permute-done | bytes 131104 | tf_op jit(solution)/shard_map/ppermute | solution.py:305
  15.9 3.8 %collective-permute-done.2.b = f32[8,32,128]{2,1,0:T(8,128)S(1)} collective-permute-done((f32[8,32,128]{2,1,0:T(8,128)S(1)}, f32[8,32,128]{2,1,0:T(8,128)S(1)}, u32[]{:S(2)}, u32[]{:S(2)}) %collective-permute-start.2) | collective-permute-done | bytes 131104 | tf_op jit(solution)/shard_map/ppermute | solution.py:305
  19.7 1.1 collective-permute-start.6
  20.8 2.3 %collective-permute-start.5 = (f32[8,32,128]{2,1,0:T(8,128)S(1)}, f32[8,32,128]{2,1,0:T(8,128)S(1)}, u32[]{:S(2)}, u32[]{:S(2)}) collective-permute-start(f32[8,32,128]{2,1,0:T(8,128)S(1)} %get-tuple-element.80.refs_0_), channel_id=1, source_target_pairs={{0,64},{32,96},{64,0},{96,32},{1,65},{33,97},{65,1},{97,33},{2,66}... | collective-permute-start | bytes 393224 | tf_op jit(solution)/shard_map/ppermute | solution.py:305
  23.9 2.3 %collective-permute-start.7 = (f32[8,32,128]{2,1,0:T(8,128)S(1)}, f32[8,32,128]{2,1,0:T(8,128)S(1)}, u32[]{:S(2)}, u32[]{:S(2)}) collective-permute-start(f32[8,32,128]{2,1,0:T(8,128)S(1)} %get-tuple-element.80.refs_0_), channel_id=1, source_target_pairs={{0,16},{16,0},{1,17},{17,1},{2,18},{18,2},{3,19},{19,3},{4,20},{20... | collective-permute-start | bytes 393224 | tf_op jit(solution)/shard_map/ppermute | solution.py:305
  26.2 2.2 %collective-permute-start.10 = (f32[8,32,128]{2,1,0:T(8,128)S(1)}, f32[8,32,128]{2,1,0:T(8,128)S(1)}, u32[]{:S(2)}, u32[]{:S(2)}) collective-permute-start(f32[8,32,128]{2,1,0:T(8,128)S(1)} %collective-permute-done.6.refs_3_), channel_id=1, source_target_pairs={{0,16},{16,0},{1,17},{17,1},{2,18},{18,2},{3,19},{19,3},{4,20},{20... | collective-permute-start | bytes 393224 | tf_op jit(solution)/shard_map/ppermute | solution.py:305
  28.4 1.9 %collective-permute-start.9 = (f32[8,32,128]{2,1,0:T(8,128)S(1)}, f32[8,32,128]{2,1,0:T(8,128)S(1)}, u32[]{:S(2)}, u32[]{:S(2)}) collective-permute-start(f32[8,32,128]{2,1,0:T(8,128)S(1)} %collective-permute-done.5.refs_2_), channel_id=1, source_target_pairs={{0,16},{16,0},{1,17},{17,1},{2,18},{18,2},{3,19},{19,3},{4,20},{20... | collective-permute-start | bytes 393224 | tf_op jit(solution)/shard_map/ppermute | solution.py:305
  31.7 5.4 %shard_map.80 = (f32[4,8,32,128]{3,2,1,0:T(8,128)S(1)}, f32[4,8,32,128]{3,2,1,0:T(8,128)S(1)}, f32[32,32,128]{2,1,0:T(8,128)S(1)}, f32[1,8,128]{2,1,0:T(8,128)S(1)}) custom-call(s32[256]{0:T(256)S(1)} %copy-done.2, s32[256]{0:T(256)S(1)} %copy-done.3, s32[3]{0:T(128)S(1)} %pad_add_fusion.me, bf16[64,128,256]{2,1,0:T(8,128)(2,1)S(1)} %get-tuple-element.72.plain, ...), custom_call_target="tpu_custom_call" | custom-call | flops 1000000 | bytes 1048576 | tf_op jit(solution)/shard_map/pallas_call | solution.py:30
  37.3 1.2 %collective-permute-start.15 = (f32[32,8,128]{2,1,0:T(8,128)S(1)}, f32[32,8,128]{2,1,0:T(8,128)S(1)}, u32[]{:S(2)}, u32[]{:S(2)}) collective-permute-start(f32[32,8,128]{2,1,0:T(8,128)S(1)} %get-tuple-element.91), channel_id=1, source_target_pairs={{0,1},{1,0},{2,3},{3,2},{4,5},{5,4},{6,7},{7,6},{8,9},{9,8},{10,11... | collective-permute-start | bytes 393224 | tf_op jit(solution)/shard_map/ppermute | solution.py:366
  39.3 1.3 %collective-permute-start.12 = (f32[8,32,128]{2,1,0:T(8,128)S(1)}, f32[8,32,128]{2,1,0:T(8,128)S(1)}, u32[]{:S(2)}, u32[]{:S(2)}) collective-permute-start(f32[8,32,128]{2,1,0:T(8,128)S(1)} %get-tuple-element.88), channel_id=1, source_target_pairs={{0,32},{32,64},{64,96},{96,0},{1,33},{33,65},{65,97},{97,1},{2,34}... | collective-permute-start | bytes 393224 | tf_op jit(solution)/shard_map/ppermute | solution.py:305
  40.6 2.1 %collective-permute-start.13 = (f32[8,32,128]{2,1,0:T(8,128)S(1)}, f32[8,32,128]{2,1,0:T(8,128)S(1)}, u32[]{:S(2)}, u32[]{:S(2)}) collective-permute-start(f32[8,32,128]{2,1,0:T(8,128)S(1)} %get-tuple-element.89), channel_id=1, source_target_pairs={{0,64},{32,96},{64,0},{96,32},{1,65},{33,97},{65,1},{97,33},{2,66}... | collective-permute-start | bytes 393224 | tf_op jit(solution)/shard_map/ppermute | solution.py:305
  43.3 1.7 %collective-permute-done.12.a = f32[8,32,128]{2,1,0:T(8,128)S(1)} collective-permute-done((f32[8,32,128]{2,1,0:T(8,128)S(1)}, f32[8,32,128]{2,1,0:T(8,128)S(1)}, u32[]{:S(2)}, u32[]{:S(2)}) %collective-permute-start.12) | collective-permute-done | bytes 131104 | tf_op jit(solution)/shard_map/ppermute | solution.py:305
  45.0 3.7 %collective-permute-done.13.b = f32[8,32,128]{2,1,0:T(8,128)S(1)} collective-permute-done((f32[8,32,128]{2,1,0:T(8,128)S(1)}, f32[8,32,128]{2,1,0:T(8,128)S(1)}, u32[]{:S(2)}, u32[]{:S(2)}) %collective-permute-start.13) | collective-permute-done | bytes 131104 | tf_op jit(solution)/shard_map/ppermute | solution.py:305
  48.8 2.0 %collective-permute-start.19 = (f32[8,32,128]{2,1,0:T(8,128)S(1)}, f32[8,32,128]{2,1,0:T(8,128)S(1)}, u32[]{:S(2)}, u32[]{:S(2)}) collective-permute-start(f32[8,32,128]{2,1,0:T(8,128)S(1)} %shard_map.82.refs_0_.sent), channel_id=1, source_target_pairs={{0,32},{32,64},{64,96},{96,0},{1,33},{33,65},{65,97},{97,1},{2,34}... | collective-permute-start | bytes 393224 | tf_op jit(solution)/shard_map/ppermute | solution.py:305
  50.8 2.0 %collective-permute-start.18 = (f32[8,32,128]{2,1,0:T(8,128)S(1)}, f32[8,32,128]{2,1,0:T(8,128)S(1)}, u32[]{:S(2)}, u32[]{:S(2)}) collective-permute-start(f32[8,32,128]{2,1,0:T(8,128)S(1)} %shard_map.82.refs_0_.sent), channel_id=1, source_target_pairs={{0,64},{32,96},{64,0},{96,32},{1,65},{33,97},{65,1},{97,33},{2,66}... | collective-permute-start | bytes 393224 | tf_op jit(solution)/shard_map/ppermute | solution.py:305
  53.3 1.5 %collective-permute-start.20 = (f32[8,32,128]{2,1,0:T(8,128)S(1)}, f32[8,32,128]{2,1,0:T(8,128)S(1)}, u32[]{:S(2)}, u32[]{:S(2)}) collective-permute-start(f32[8,32,128]{2,1,0:T(8,128)S(1)} %shard_map.82.refs_0_.sent), channel_id=1, source_target_pairs={{0,16},{16,0},{1,17},{17,1},{2,18},{18,2},{3,19},{19,3},{4,20},{20... | collective-permute-start | bytes 393224 | tf_op jit(solution)/shard_map/ppermute | solution.py:305
  54.8 1.9 %collective-permute-start.23 = (f32[8,32,128]{2,1,0:T(8,128)S(1)}, f32[8,32,128]{2,1,0:T(8,128)S(1)}, u32[]{:S(2)}, u32[]{:S(2)}) collective-permute-start(f32[8,32,128]{2,1,0:T(8,128)S(1)} %collective-permute-done.19.refs_3_), channel_id=1, source_target_pairs={{0,16},{16,0},{1,17},{17,1},{2,18},{18,2},{3,19},{19,3},{4,20},{20... | collective-permute-start | bytes 393224 | tf_op jit(solution)/shard_map/ppermute | solution.py:305
  56.7 1.7 %collective-permute-done.18.refs_2_ = f32[8,32,128]{2,1,0:T(8,128)S(1)} collective-permute-done((f32[8,32,128]{2,1,0:T(8,128)S(1)}, f32[8,32,128]{2,1,0:T(8,128)S(1)}, u32[]{:S(2)}, u32[]{:S(2)}) %collective-permute-start.18) | collective-permute-done | bytes 131104 | tf_op jit(solution)/shard_map/ppermute | solution.py:305
  58.4 1.7 %collective-permute-start.22 = (f32[8,32,128]{2,1,0:T(8,128)S(1)}, f32[8,32,128]{2,1,0:T(8,128)S(1)}, u32[]{:S(2)}, u32[]{:S(2)}) collective-permute-start(f32[8,32,128]{2,1,0:T(8,128)S(1)} %collective-permute-done.18.refs_2_), channel_id=1, source_target_pairs={{0,16},{16,0},{1,17},{17,1},{2,18},{18,2},{3,19},{19,3},{4,20},{20... | collective-permute-start | bytes 393224 | tf_op jit(solution)/shard_map/ppermute | solution.py:305
  61.4 6.0 %shard_map.83 = (f32[4,8,32,128]{3,2,1,0:T(8,128)S(1)}, f32[4,8,32,128]{3,2,1,0:T(8,128)S(1)}, f32[32,32,128]{2,1,0:T(8,128)}, f32[2,8,128]{2,1,0:T(8,128)S(1)},...) custom-call(s32[256]{0:T(256)S(1)} %copy-done.2, s32[256]{0:T(256)S(1)} %copy-done.3, s32[3]{0:T(128)S(1)} %pad_add_fusion.me, ...), custom_call_target="tpu_custom_call" | custom-call | flops 1000000 | bytes 1048576 | tf_op jit(solution)/shard_map/pallas_call | solution.py:30
  67.6 1.7 %collective-permute-done.24.got = f32[4,8,32,128]{3,2,1,0:T(8,128)S(1)} collective-permute-done((f32[4,8,32,128]{3,2,1,0:T(8,128)S(1)}, f32[4,8,32,128]{3,2,1,0:T(8,128)S(1)}, u32[]{:S(2)}, u32[]{:S(2)}) %collective-permute-start.24) | collective-permute-done | bytes 524320 | tf_op jit(solution)/shard_map/ppermute | solution.py:305
  70.1 2.1 %collective-permute-start.26 = (f32[8,32,128]{2,1,0:T(8,128)S(1)}, f32[8,32,128]{2,1,0:T(8,128)S(1)}, u32[]{:S(2)}, u32[]{:S(2)}) collective-permute-start(f32[8,32,128]{2,1,0:T(8,128)S(1)} %get-tuple-element.102), channel_id=1, source_target_pairs={{0,64},{32,96},{64,0},{96,32},{1,65},{33,97},{65,1},{97,33},{2,66}... | collective-permute-start | bytes 393224 | tf_op jit(solution)/shard_map/ppermute | solution.py:305
  72.9 3.1 %collective-permute-start.28 = (f32[32,8,128]{2,1,0:T(8,128)S(1)}, f32[32,8,128]{2,1,0:T(8,128)S(1)}, u32[]{:S(2)}, u32[]{:S(2)}) collective-permute-start(f32[32,8,128]{2,1,0:T(8,128)S(1)} %get-tuple-element.109), channel_id=1, source_target_pairs={{0,1},{1,0},{2,3},{3,2},{4,5},{5,4},{6,7},{7,6},{8,9},{9,8},{10,11... | collective-permute-start | bytes 393224 | tf_op jit(solution)/shard_map/ppermute | solution.py:379
  76.8 1.4 %collective-permute-done.26.b = f32[8,32,128]{2,1,0:T(8,128)S(1)} collective-permute-done((f32[8,32,128]{2,1,0:T(8,128)S(1)}, f32[8,32,128]{2,1,0:T(8,128)S(1)}, u32[]{:S(2)}, u32[]{:S(2)}) %collective-permute-start.26) | collective-permute-done | bytes 131104 | tf_op jit(solution)/shard_map/ppermute | solution.py:305
  78.7 1.1 %shard_map.86 = (f32[8,32,128]{2,1,0:T(8,128)S(1)}, f32[128,128]{1,0:T(8,128)S(1)}) custom-call(f32[8,32,128]{2,1,0:T(8,128)S(1)} %get-tuple-element.100.kept, f32[8,32,128]{2,1,0:T(8,128)S(1)} %collective-permute-done.25.a, f32[8,32,128]{2,1,0:T(8,128)S(1)} %collective-permute-done.26.b, f32[8,32,128]{2,1,0:T(8,128)S(1)} %collective-permute-done.27.c, ...), custom_call_target="tpu_custom_call" | custom-call | flops 1000000 | bytes 1048576 | tf_op jit(solution)/shard_map/pallas_call | solution.py:30
  79.8 23.1 %all_to_all.20 = f32[128,1,128]{2,1,0:T(1,128)S(1)} all-to-all(f32[128,1,128]{2,1,0:T(1,128)S(1)} %bitcast.18), channel_id=1, replica_groups=mesh['tile_0'=4,'tile_1'=2,'slab_0'=4,'slab_1'=4] {'tile_0','tile_1','sl..., dimensions={0} | all-to-all | bytes 131072 | tf_op jit(solution)/shard_map/all_to_all | solution.py:323
  105.1 2.8 %shard_map.88 = (f32[32,4096]{1,0:T(8,128)}, f32[32,1024]{1,0:T(8,128)}) custom-call(s32[3]{0:T(128)S(1)} %add_convert_fusion.ends, f32[3]{0:T(128)S(1)} %get-tuple-element.120.alphas, f32[32,4096]{1,0:T(8,128)S(1)} %copy-done, f32[32,32,128]{2,1,0:T(8,128)S(1)} %get-tuple-element.97.refs_8_.grad, f32[32,32,128]{2,1,0:T(8,128)} %get-tuple-element.114.turned, ...), custom_call_target="tpu_custom_call" | custom-call | flops 1000000 | bytes 1048576 | tf_op jit(solution)/shard_map/pallas_call | solution.py:30
  (57 shorter events, 11.3 us)
Async XLA Ops:
  0.6 31.0 %copy-start.3 = (s32[256]{0:T(256)S(1)}, s32[256]{0:T(256)}, u32[]{:S(2)}) copy-start(s32[256]{0:T(256)} %strips.3) | copy-start | bytes 3076
  6.5 3.0 %collective-permute-start = (f32[4,8,32,128]{3,2,1,0:T(8,128)S(1)}, f32[4,8,32,128]{3,2,1,0:T(8,128)S(1)}, u32[]{:S(2)}, u32[]{:S(2)}) collective-permute-start(f32[4,8,32,128]{3,2,1,0:T(8,128)S(1)} %get-tuple-element.75), channel_id=1, source_target_pairs={{0,16},{16,0},{1,17},{17,1},{2,18},{18,2},{3,19},{19,3},{4,20},{20... | collective-permute-start | bytes 1572872 | tf_op jit(solution)/shard_map/ppermute | solution.py:305
  9.6 6.3 %collective-permute-start.1 = (f32[8,32,128]{2,1,0:T(8,128)S(1)}, f32[8,32,128]{2,1,0:T(8,128)S(1)}, u32[]{:S(2)}, u32[]{:S(2)}) collective-permute-start(f32[8,32,128]{2,1,0:T(8,128)S(1)} %get-tuple-element.77), channel_id=1, source_target_pairs={{0,32},{32,64},{64,96},{96,0},{1,33},{33,65},{65,97},{97,1},{2,34}... | collective-permute-start | bytes 393224 | tf_op jit(solution)/shard_map/ppermute | solution.py:305
  11.0 8.7 %collective-permute-start.2 = (f32[8,32,128]{2,1,0:T(8,128)S(1)}, f32[8,32,128]{2,1,0:T(8,128)S(1)}, u32[]{:S(2)}, u32[]{:S(2)}) collective-permute-start(f32[8,32,128]{2,1,0:T(8,128)S(1)} %get-tuple-element.78), channel_id=1, source_target_pairs={{0,64},{32,96},{64,0},{96,32},{1,65},{33,97},{65,1},{97,33},{2,66}... | collective-permute-start | bytes 393224 | tf_op jit(solution)/shard_map/ppermute | solution.py:305
  13.7 6.0 %collective-permute-start.3 = (f32[8,32,128]{2,1,0:T(8,128)S(1)}, f32[8,32,128]{2,1,0:T(8,128)S(1)}, u32[]{:S(2)}, u32[]{:S(2)}) collective-permute-start(f32[8,32,128]{2,1,0:T(8,128)S(1)} %get-tuple-element.79), channel_id=1, source_target_pairs={{0,96},{32,0},{64,32},{96,64},{1,97},{33,1},{65,33},{97,65},{2,98}... | collective-permute-start | bytes 393224 | tf_op jit(solution)/shard_map/ppermute | solution.py:305
  19.7 6.5 %collective-permute-start.6 = (f32[8,32,128]{2,1,0:T(8,128)S(1)}, f32[8,32,128]{2,1,0:T(8,128)S(1)}, u32[]{:S(2)}, u32[]{:S(2)}) collective-permute-start(f32[8,32,128]{2,1,0:T(8,128)S(1)} %get-tuple-element.80.refs_0_), channel_id=1, source_target_pairs={{0,32},{32,64},{64,96},{96,0},{1,33},{33,65},{65,97},{97,1},{2,34}... | collective-permute-start | bytes 393224 | tf_op jit(solution)/shard_map/ppermute | solution.py:305
  20.8 7.6 %collective-permute-start.5 = (f32[8,32,128]{2,1,0:T(8,128)S(1)}, f32[8,32,128]{2,1,0:T(8,128)S(1)}, u32[]{:S(2)}, u32[]{:S(2)}) collective-permute-start(f32[8,32,128]{2,1,0:T(8,128)S(1)} %get-tuple-element.80.refs_0_), channel_id=1, source_target_pairs={{0,64},{32,96},{64,0},{96,32},{1,65},{33,97},{65,1},{97,33},{2,66}... | collective-permute-start | bytes 393224 | tf_op jit(solution)/shard_map/ppermute | solution.py:305
  23.1 7.3 %collective-permute-start.4 = (f32[8,32,128]{2,1,0:T(8,128)S(1)}, f32[8,32,128]{2,1,0:T(8,128)S(1)}, u32[]{:S(2)}, u32[]{:S(2)}) collective-permute-start(f32[8,32,128]{2,1,0:T(8,128)S(1)} %get-tuple-element.80.refs_0_), channel_id=1, source_target_pairs={{0,96},{32,0},{64,32},{96,64},{1,97},{33,1},{65,33},{97,65},{2,98}... | collective-permute-start | bytes 393224 | tf_op jit(solution)/shard_map/ppermute | solution.py:305
  23.9 6.5 %collective-permute-start.7 = (f32[8,32,128]{2,1,0:T(8,128)S(1)}, f32[8,32,128]{2,1,0:T(8,128)S(1)}, u32[]{:S(2)}, u32[]{:S(2)}) collective-permute-start(f32[8,32,128]{2,1,0:T(8,128)S(1)} %get-tuple-element.80.refs_0_), channel_id=1, source_target_pairs={{0,16},{16,0},{1,17},{17,1},{2,18},{18,2},{3,19},{19,3},{4,20},{20... | collective-permute-start | bytes 393224 | tf_op jit(solution)/shard_map/ppermute | solution.py:305
  26.2 4.2 %collective-permute-start.10 = (f32[8,32,128]{2,1,0:T(8,128)S(1)}, f32[8,32,128]{2,1,0:T(8,128)S(1)}, u32[]{:S(2)}, u32[]{:S(2)}) collective-permute-start(f32[8,32,128]{2,1,0:T(8,128)S(1)} %collective-permute-done.6.refs_3_), channel_id=1, source_target_pairs={{0,16},{16,0},{1,17},{17,1},{2,18},{18,2},{3,19},{19,3},{4,20},{20... | collective-permute-start | bytes 393224 | tf_op jit(solution)/shard_map/ppermute | solution.py:305
  28.4 2.9 %collective-permute-start.9 = (f32[8,32,128]{2,1,0:T(8,128)S(1)}, f32[8,32,128]{2,1,0:T(8,128)S(1)}, u32[]{:S(2)}, u32[]{:S(2)}) collective-permute-start(f32[8,32,128]{2,1,0:T(8,128)S(1)} %collective-permute-done.5.refs_2_), channel_id=1, source_target_pairs={{0,16},{16,0},{1,17},{17,1},{2,18},{18,2},{3,19},{19,3},{4,20},{20... | collective-permute-start | bytes 393224 | tf_op jit(solution)/shard_map/ppermute | solution.py:305
  30.3 1.3 %collective-permute-start.8 = (f32[8,32,128]{2,1,0:T(8,128)S(1)}, f32[8,32,128]{2,1,0:T(8,128)S(1)}, u32[]{:S(2)}, u32[]{:S(2)}) collective-permute-start(f32[8,32,128]{2,1,0:T(8,128)S(1)} %collective-permute-done.4.refs_1_), channel_id=1, source_target_pairs={{0,16},{16,0},{1,17},{17,1},{2,18},{18,2},{3,19},{19,3},{4,20},{20... | collective-permute-start | bytes 393224 | tf_op jit(solution)/shard_map/ppermute | solution.py:305
  37.1 2.1 %collective-permute-start.11 = (f32[4,8,32,128]{3,2,1,0:T(8,128)S(1)}, f32[4,8,32,128]{3,2,1,0:T(8,128)S(1)}, u32[]{:S(2)}, u32[]{:S(2)}) collective-permute-start(f32[4,8,32,128]{3,2,1,0:T(8,128)S(1)} %get-tuple-element.86), channel_id=1, source_target_pairs={{0,16},{16,0},{1,17},{17,1},{2,18},{18,2},{3,19},{19,3},{4,20},{20... | collective-permute-start | bytes 1572872 | tf_op jit(solution)/shard_map/ppermute | solution.py:305
  37.3 6.0 %collective-permute-start.15 = (f32[32,8,128]{2,1,0:T(8,128)S(1)}, f32[32,8,128]{2,1,0:T(8,128)S(1)}, u32[]{:S(2)}, u32[]{:S(2)}) collective-permute-start(f32[32,8,128]{2,1,0:T(8,128)S(1)} %get-tuple-element.91), channel_id=1, source_target_pairs={{0,1},{1,0},{2,3},{3,2},{4,5},{5,4},{6,7},{7,6},{8,9},{9,8},{10,11... | collective-permute-start | bytes 393224 | tf_op jit(solution)/shard_map/ppermute | solution.py:366
  38.6 4.8 %collective-permute-start.16 = (f32[32,8,128]{2,1,0:T(8,128)S(1)}, f32[32,8,128]{2,1,0:T(8,128)S(1)}, u32[]{:S(2)}, u32[]{:S(2)}) collective-permute-start(f32[32,8,128]{2,1,0:T(8,128)S(1)} %get-tuple-element.92), channel_id=1, source_target_pairs={{0,0},{1,2},{2,1},{3,4},{4,3},{5,6},{6,5},{7,8},{8,7},{9,10},{10,9... | collective-permute-start | bytes 393224 | tf_op jit(solution)/shard_map/ppermute | solution.py:366
  39.3 5.7 %collective-permute-start.12 = (f32[8,32,128]{2,1,0:T(8,128)S(1)}, f32[8,32,128]{2,1,0:T(8,128)S(1)}, u32[]{:S(2)}, u32[]{:S(2)}) collective-permute-start(f32[8,32,128]{2,1,0:T(8,128)S(1)} %get-tuple-element.88), channel_id=1, source_target_pairs={{0,32},{32,64},{64,96},{96,0},{1,33},{33,65},{65,97},{97,1},{2,34}... | collective-permute-start | bytes 393224 | tf_op jit(solution)/shard_map/ppermute | solution.py:305
  40.6 8.1 %collective-permute-start.13 = (f32[8,32,128]{2,1,0:T(8,128)S(1)}, f32[8,32,128]{2,1,0:T(8,128)S(1)}, u32[]{:S(2)}, u32[]{:S(2)}) collective-permute-start(f32[8,32,128]{2,1,0:T(8,128)S(1)} %get-tuple-element.89), channel_id=1, source_target_pairs={{0,64},{32,96},{64,0},{96,32},{1,65},{33,97},{65,1},{97,33},{2,66}... | collective-permute-start | bytes 393224 | tf_op jit(solution)/shard_map/ppermute | solution.py:305
  42.8 6.0 %collective-permute-start.14 = (f32[8,32,128]{2,1,0:T(8,128)S(1)}, f32[8,32,128]{2,1,0:T(8,128)S(1)}, u32[]{:S(2)}, u32[]{:S(2)}) collective-permute-start(f32[8,32,128]{2,1,0:T(8,128)S(1)} %get-tuple-element.90), channel_id=1, source_target_pairs={{0,96},{32,0},{64,32},{96,64},{1,97},{33,1},{65,33},{97,65},{2,98}... | collective-permute-start | bytes 393224 | tf_op jit(solution)/shard_map/ppermute | solution.py:305
  48.8 6.0 %collective-permute-start.19 = (f32[8,32,128]{2,1,0:T(8,128)S(1)}, f32[8,32,128]{2,1,0:T(8,128)S(1)}, u32[]{:S(2)}, u32[]{:S(2)}) collective-permute-start(f32[8,32,128]{2,1,0:T(8,128)S(1)} %shard_map.82.refs_0_.sent), channel_id=1, source_target_pairs={{0,32},{32,64},{64,96},{96,0},{1,33},{33,65},{65,97},{97,1},{2,34}... | collective-permute-start | bytes 393224 | tf_op jit(solution)/shard_map/ppermute | solution.py:305
  50.8 7.6 %collective-permute-start.18 = (f32[8,32,128]{2,1,0:T(8,128)S(1)}, f32[8,32,128]{2,1,0:T(8,128)S(1)}, u32[]{:S(2)}, u32[]{:S(2)}) collective-permute-start(f32[8,32,128]{2,1,0:T(8,128)S(1)} %shard_map.82.refs_0_.sent), channel_id=1, source_target_pairs={{0,64},{32,96},{64,0},{96,32},{1,65},{33,97},{65,1},{97,33},{2,66}... | collective-permute-start | bytes 393224 | tf_op jit(solution)/shard_map/ppermute | solution.py:305
  52.8 7.3 %collective-permute-start.17 = (f32[8,32,128]{2,1,0:T(8,128)S(1)}, f32[8,32,128]{2,1,0:T(8,128)S(1)}, u32[]{:S(2)}, u32[]{:S(2)}) collective-permute-start(f32[8,32,128]{2,1,0:T(8,128)S(1)} %shard_map.82.refs_0_.sent), channel_id=1, source_target_pairs={{0,96},{32,0},{64,32},{96,64},{1,97},{33,1},{65,33},{97,65},{2,98}... | collective-permute-start | bytes 393224 | tf_op jit(solution)/shard_map/ppermute | solution.py:305
  53.3 6.8 %collective-permute-start.20 = (f32[8,32,128]{2,1,0:T(8,128)S(1)}, f32[8,32,128]{2,1,0:T(8,128)S(1)}, u32[]{:S(2)}, u32[]{:S(2)}) collective-permute-start(f32[8,32,128]{2,1,0:T(8,128)S(1)} %shard_map.82.refs_0_.sent), channel_id=1, source_target_pairs={{0,16},{16,0},{1,17},{17,1},{2,18},{18,2},{3,19},{19,3},{4,20},{20... | collective-permute-start | bytes 393224 | tf_op jit(solution)/shard_map/ppermute | solution.py:305
  54.8 5.3 %collective-permute-start.23 = (f32[8,32,128]{2,1,0:T(8,128)S(1)}, f32[8,32,128]{2,1,0:T(8,128)S(1)}, u32[]{:S(2)}, u32[]{:S(2)}) collective-permute-start(f32[8,32,128]{2,1,0:T(8,128)S(1)} %collective-permute-done.19.refs_3_), channel_id=1, source_target_pairs={{0,16},{16,0},{1,17},{17,1},{2,18},{18,2},{3,19},{19,3},{4,20},{20... | collective-permute-start | bytes 393224 | tf_op jit(solution)/shard_map/ppermute | solution.py:305
  58.4 2.6 %collective-permute-start.22 = (f32[8,32,128]{2,1,0:T(8,128)S(1)}, f32[8,32,128]{2,1,0:T(8,128)S(1)}, u32[]{:S(2)}, u32[]{:S(2)}) collective-permute-start(f32[8,32,128]{2,1,0:T(8,128)S(1)} %collective-permute-done.18.refs_2_), channel_id=1, source_target_pairs={{0,16},{16,0},{1,17},{17,1},{2,18},{18,2},{3,19},{19,3},{4,20},{20... | collective-permute-start | bytes 393224 | tf_op jit(solution)/shard_map/ppermute | solution.py:305
  60.0 1.3 %collective-permute-start.21 = (f32[8,32,128]{2,1,0:T(8,128)S(1)}, f32[8,32,128]{2,1,0:T(8,128)S(1)}, u32[]{:S(2)}, u32[]{:S(2)}) collective-permute-start(f32[8,32,128]{2,1,0:T(8,128)S(1)} %collective-permute-done.17.refs_1_), channel_id=1, source_target_pairs={{0,16},{16,0},{1,17},{17,1},{2,18},{18,2},{3,19},{19,3},{4,20},{20... | collective-permute-start | bytes 393224 | tf_op jit(solution)/shard_map/ppermute | solution.py:305
  67.4 37.6 %copy-start = (f32[32,4096]{1,0:T(8,128)S(1)}, f32[32,4096]{1,0:T(8,128)}, u32[]{:S(2)}) copy-start(f32[32,4096]{1,0:T(8,128)} %volume.1) | copy-start | bytes 1572868
  67.4 1.9 %collective-permute-start.24 = (f32[4,8,32,128]{3,2,1,0:T(8,128)S(1)}, f32[4,8,32,128]{3,2,1,0:T(8,128)S(1)}, u32[]{:S(2)}, u32[]{:S(2)}) collective-permute-start(f32[4,8,32,128]{3,2,1,0:T(8,128)S(1)} %get-tuple-element.99), channel_id=1, source_target_pairs={{0,16},{16,0},{1,17},{17,1},{2,18},{18,2},{3,19},{19,3},{4,20},{20... | collective-permute-start | bytes 1572872 | tf_op jit(solution)/shard_map/ppermute | solution.py:305
  69.4 7.4 %collective-permute-start.25 = (f32[8,32,128]{2,1,0:T(8,128)S(1)}, f32[8,32,128]{2,1,0:T(8,128)S(1)}, u32[]{:S(2)}, u32[]{:S(2)}) collective-permute-start(f32[8,32,128]{2,1,0:T(8,128)S(1)} %get-tuple-element.101), channel_id=1, source_target_pairs={{0,32},{32,64},{64,96},{96,0},{1,33},{33,65},{65,97},{97,1},{2,34}... | collective-permute-start | bytes 393224 | tf_op jit(solution)/shard_map/ppermute | solution.py:305
  70.1 8.1 %collective-permute-start.26 = (f32[8,32,128]{2,1,0:T(8,128)S(1)}, f32[8,32,128]{2,1,0:T(8,128)S(1)}, u32[]{:S(2)}, u32[]{:S(2)}) collective-permute-start(f32[8,32,128]{2,1,0:T(8,128)S(1)} %get-tuple-element.102), channel_id=1, source_target_pairs={{0,64},{32,96},{64,0},{96,32},{1,65},{33,97},{65,1},{97,33},{2,66}... | collective-permute-start | bytes 393224 | tf_op jit(solution)/shard_map/ppermute | solution.py:305
  72.2 6.5 %collective-permute-start.27 = (f32[8,32,128]{2,1,0:T(8,128)S(1)}, f32[8,32,128]{2,1,0:T(8,128)S(1)}, u32[]{:S(2)}, u32[]{:S(2)}) collective-permute-start(f32[8,32,128]{2,1,0:T(8,128)S(1)} %get-tuple-element.103), channel_id=1, source_target_pairs={{0,96},{32,0},{64,32},{96,64},{1,97},{33,1},{65,33},{97,65},{2,98}... | collective-permute-start | bytes 393224 | tf_op jit(solution)/shard_map/ppermute | solution.py:305
  72.9 6.9 %collective-permute-start.28 = (f32[32,8,128]{2,1,0:T(8,128)S(1)}, f32[32,8,128]{2,1,0:T(8,128)S(1)}, u32[]{:S(2)}, u32[]{:S(2)}) collective-permute-start(f32[32,8,128]{2,1,0:T(8,128)S(1)} %get-tuple-element.109), channel_id=1, source_target_pairs={{0,1},{1,0},{2,3},{3,2},{4,5},{5,4},{6,7},{7,6},{8,9},{9,8},{10,11... | collective-permute-start | bytes 393224 | tf_op jit(solution)/shard_map/ppermute | solution.py:379
  76.0 3.8 %collective-permute-start.29 = (f32[32,8,128]{2,1,0:T(8,128)S(1)}, f32[32,8,128]{2,1,0:T(8,128)S(1)}, u32[]{:S(2)}, u32[]{:S(2)}) collective-permute-start(f32[32,8,128]{2,1,0:T(8,128)S(1)} %get-tuple-element.110), channel_id=1, source_target_pairs={{0,0},{1,2},{2,1},{3,4},{4,3},{5,6},{6,5},{7,8},{8,7},{9,10},{10,9... | collective-permute-start | bytes 393224 | tf_op jit(solution)/shard_map/ppermute | solution.py:379
  (4 other events, 97.3 us)

commit v2 on v0

--- a/solution.py
+++ b/solution.py
@@ -199,12 +199,14 @@
     sent[...] = tile_cols(weights) * value
 
 
-def middle_kernel(kept, a, b, c, weights, projected, sent, sums):
+def resend_kernel(kept, a, b, c, weights, sent):
+    sent[...] = tile_cols(weights) * (kept[...] + a[...] + b[...] + c[...])
+
+
+def middle_kernel(kept, a, b, c, sent, projected, sums):
     value = kept[...] + a[...] + b[...] + c[...]
-    weighted = tile_cols(weights) * value
     projected[...] = value
-    sent[...] = weighted
-    sums[0] = folded(weighted * value)
+    sums[0] = folded(sent[...] * value)
 
 
 def in_lanes(sums, shape):
@@ -349,13 +351,15 @@
     mine, theirs, first0, last0 = lax.optimization_barrier((mine, theirs, first0, last0))
     parts = summed_by_owner(mine, theirs)
     first0, last0 = lax.ppermute(first0, SLAB, down), lax.ppermute(last0, SLAB, up)
-    parts, first0, last0 = lax.optimization_barrier((parts, first0, last0))
-    p0, sent, curve0 = call(middle_kernel, [RAY, RAY, tile], [*parts, weights])
+    sent = call(resend_kernel, [RAY], [*parts, weights])[0]
+    p0, curve0 = call(middle_kernel, [RAY, tile], [*parts, sent])
+    pieces = to_everyone(sent)
+    pieces, first0, last0 = lax.optimization_barrier((pieces, first0, last0))
 
     mine, theirs, back, crossed, first, last = call(
         third_kernel,
         [half, half, field, (2, 8, 128), edge, edge],
-        [*spots, plain, turned, *to_everyone(sent), grad],
+        [*spots, plain, turned, *pieces, grad],
         scratch,
         3,
     )
@@ -365,7 +369,7 @@
     q0, rows = call(
         end_kernel, [RAY, (everyone, 128)], [*parts, weights, p0, norm0, curve0, crossed]
     )
-    rows, first, last, ends = lax.optimization_barrier((rows, first, last, ends))
+    rows, ends = lax.optimization_barrier((rows, ends))
     rows = over_all(rows)
     alphas, again = pl.pallas_call(
         judge_kernel,

time: 108 us -> 105 us (0.972)
  waiting for transfers between devices: 23.9 us -> 15.7 us
  blocking collectives: 15.3 us -> 18.8 us
    ppermute x1, waiting for transfers between devices: 4.63 us -> 0.01 us  [shards(): lax.ppermute(last, SLAB, up)]
    all_to_all x1, blocking collectives: 15.3 us -> 18.8 us  [over_all(): return lax.all_to_all(rows, TILE + SLAB, 0, 0, tiled=True)]
    ppermute x1, waiting for transfers between devices: 3.68 us -> 1.03 us  [shards(): lax.ppermute(last0, SLAB, up)]
    ppermute x1, starting transfers between devices: 4.53 us -> 3.29 us  [shards(): lax.ppermute(first, SLAB, down)]
    ppermute x1, starting transfers between devices: 0.01 us -> 1.21 us  [shards(): lax.ppermute(last0, SLAB, up)]
    ppermute x26, starting transfers between devices: 34.7 us -> 35.8 us  [shift(): return lax.ppermute(value, axis, [(i, (i + by) % n) for i in range(n)])]
    pallas_call x10 -> x11, Pallas kernels: 21.3 us -> 21.3 us  [call(): pl.pallas_call(kernel, out_shape=[s if hasattr(s, 'dtype') else jax.Shape...]
  transfers between devices with their start and end apart: 30 -> 30, of which waited for: 14 -> 12; matrix products, arithmetic and copies ran while one was open for 0% -> 0% of each run, Pallas kernels for 1% -> 2%
where the time goes in v2:
time: 105 us
  starting transfers between devices  46.2 us (44%)
  Pallas kernels  22.2 us (21%)
  blocking collectives  18.8 us (18%)
  waiting for transfers between devices  15.7 us (15%)
  between operations  1.45 us (1%)
    ppermute x26, starting transfers between devices, shift(): return lax.ppermute(value, axis, [(i, (i + by) % n) for i in range(n)])  35.8 us
    pallas_call x11, Pallas kernels, call(): pl.pallas_call(kernel, out_shape=[s if hasattr(s, 'dtype') else jax.Shape...  21.3 us
    all_to_all x1, blocking collectives, over_all(): return lax.all_to_all(rows, TILE + SLAB, 0, 0, tiled=True)  18.8 us
    ppermute x26, waiting for transfers between devices, shift(): return lax.ppermute(value, axis, [(i, (i + by) % n) for i in range(n)])  14.7 us
    ppermute x1, starting transfers between devices, shards(): lax.ppermute(first0, SLAB, down)  5.95 us
    ppermute x1, starting transfers between devices, shards(): lax.ppermute(first, SLAB, down)  3.29 us
  transfers between devices with their start and end apart: 30, of which 12 were waited for; matrix products, arithmetic and copies ran while one was open for 0% of the time, Pallas kernels for 2%

profile of v2, /device:TPU:1, one launch (start us, length us, event | category | flops | bytes accessed | tf_op | source)
XLA Modules:
  0.0 104.5 jit_solution(10832676983115387196)
XLA Ops:
  0.8 5.7 %shard_map.77 = (f32[4,8,32,128]{3,2,1,0:T(8,128)S(1)}, f32[4,8,32,128]{3,2,1,0:T(8,128)S(1)}, f32[32,8,128]{2,1,0:T(8,128)S(1)}, f32[32,8,128]{2,1,0:T(8,128)S(...) custom-call(s32[256]{0:T(256)} %pixels.3, s32[256]{0:T(256)} %strips.3, s32[2]{0:T(128)S(1)} %pad_add_fusion.me, ...), custom_call_target="tpu_custom_call" | custom-call | flops 1000000 | bytes 1048576 | tf_op jit(solution)/shard_map/pallas_call | solution.py:30
  6.5 1.5 %collective-permute-start = (f32[4,8,32,128]{3,2,1,0:T(8,128)S(1)}, f32[4,8,32,128]{3,2,1,0:T(8,128)S(1)}, u32[]{:S(2)}, u32[]{:S(2)}) collective-permute-start(f32[4,8,32,128]{3,2,1,0:T(8,128)S(1)} %get-tuple-element.79), channel_id=1, source_target_pairs={{0,16},{16,0},{1,17},{17,1},{2,18},{18,2},{3,19},{19,3},{4,20},{20... | collective-permute-start | bytes 1572872 | tf_op jit(solution)/shard_map/ppermute | solution.py:292
  8.0 1.5 %collective-permute-done.got = f32[4,8,32,128]{3,2,1,0:T(8,128)S(1)} collective-permute-done((f32[4,8,32,128]{3,2,1,0:T(8,128)S(1)}, f32[4,8,32,128]{3,2,1,0:T(8,128)S(1)}, u32[]{:S(2)}, u32[]{:S(2)}) %collective-permute-start) | collective-permute-done | bytes 524320 | tf_op jit(solution)/shard_map/ppermute | solution.py:292
  9.5 1.5 %collective-permute-start.1 = (f32[8,32,128]{2,1,0:T(8,128)S(1)}, f32[8,32,128]{2,1,0:T(8,128)S(1)}, u32[]{:S(2)}, u32[]{:S(2)}) collective-permute-start(f32[8,32,128]{2,1,0:T(8,128)S(1)} %get-tuple-element.81), channel_id=1, source_target_pairs={{0,32},{32,64},{64,96},{96,0},{1,33},{33,65},{65,97},{97,1},{2,34}... | collective-permute-start | bytes 393224 | tf_op jit(solution)/shard_map/ppermute | solution.py:292
  11.0 2.6 %collective-permute-start.2 = (f32[8,32,128]{2,1,0:T(8,128)S(1)}, f32[8,32,128]{2,1,0:T(8,128)S(1)}, u32[]{:S(2)}, u32[]{:S(2)}) collective-permute-start(f32[8,32,128]{2,1,0:T(8,128)S(1)} %get-tuple-element.82), channel_id=1, source_target_pairs={{0,64},{32,96},{64,0},{96,32},{1,65},{33,97},{65,1},{97,33},{2,66}... | collective-permute-start | bytes 393224 | tf_op jit(solution)/shard_map/ppermute | solution.py:292
  14.7 1.1 %collective-permute-done.1.a = f32[8,32,128]{2,1,0:T(8,128)S(1)} collective-permute-done((f32[8,32,128]{2,1,0:T(8,128)S(1)}, f32[8,32,128]{2,1,0:T(8,128)S(1)}, u32[]{:S(2)}, u32[]{:S(2)}) %collective-permute-start.1) | collective-permute-done | bytes 131104 | tf_op jit(solution)/shard_map/ppermute | solution.py:292
  15.9 3.8 %collective-permute-done.2.b = f32[8,32,128]{2,1,0:T(8,128)S(1)} collective-permute-done((f32[8,32,128]{2,1,0:T(8,128)S(1)}, f32[8,32,128]{2,1,0:T(8,128)S(1)}, u32[]{:S(2)}, u32[]{:S(2)}) %collective-permute-start.2) | collective-permute-done | bytes 131104 | tf_op jit(solution)/shard_map/ppermute | solution.py:292
  20.8 2.3 %collective-permute-start.5 = (f32[8,32,128]{2,1,0:T(8,128)S(1)}, f32[8,32,128]{2,1,0:T(8,128)S(1)}, u32[]{:S(2)}, u32[]{:S(2)}) collective-permute-start(f32[8,32,128]{2,1,0:T(8,128)S(1)} %get-tuple-element.84.refs_0_), channel_id=1, source_target_pairs={{0,64},{32,96},{64,0},{96,32},{1,65},{33,97},{65,1},{97,33},{2,66}... | collective-permute-start | bytes 393224 | tf_op jit(solution)/shard_map/ppermute | solution.py:292
  23.9 2.3 %collective-permute-start.7 = (f32[8,32,128]{2,1,0:T(8,128)S(1)}, f32[8,32,128]{2,1,0:T(8,128)S(1)}, u32[]{:S(2)}, u32[]{:S(2)}) collective-permute-start(f32[8,32,128]{2,1,0:T(8,128)S(1)} %get-tuple-element.84.refs_0_), channel_id=1, source_target_pairs={{0,16},{16,0},{1,17},{17,1},{2,18},{18,2},{3,19},{19,3},{4,20},{20... | collective-permute-start | bytes 393224 | tf_op jit(solution)/shard_map/ppermute | solution.py:292
  26.2 2.2 %collective-permute-start.10 = (f32[8,32,128]{2,1,0:T(8,128)S(1)}, f32[8,32,128]{2,1,0:T(8,128)S(1)}, u32[]{:S(2)}, u32[]{:S(2)}) collective-permute-start(f32[8,32,128]{2,1,0:T(8,128)S(1)} %collective-permute-done.6.refs_3_), channel_id=1, source_target_pairs={{0,16},{16,0},{1,17},{17,1},{2,18},{18,2},{3,19},{19,3},{4,20},{20... | collective-permute-start | bytes 393224 | tf_op jit(solution)/shard_map/ppermute | solution.py:292
  28.4 1.9 %collective-permute-start.9 = (f32[8,32,128]{2,1,0:T(8,128)S(1)}, f32[8,32,128]{2,1,0:T(8,128)S(1)}, u32[]{:S(2)}, u32[]{:S(2)}) collective-permute-start(f32[8,32,128]{2,1,0:T(8,128)S(1)} %collective-permute-done.5.refs_2_), channel_id=1, source_target_pairs={{0,16},{16,0},{1,17},{17,1},{2,18},{18,2},{3,19},{19,3},{4,20},{20... | collective-permute-start | bytes 393224 | tf_op jit(solution)/shard_map/ppermute | solution.py:292
  31.7 5.4 %shard_map.80 = (f32[4,8,32,128]{3,2,1,0:T(8,128)S(1)}, f32[4,8,32,128]{3,2,1,0:T(8,128)S(1)}, f32[32,32,128]{2,1,0:T(8,128)S(1)}, f32[1,8,128]{2,1,0:T(8,128)S(1)}) custom-call(s32[256]{0:T(256)S(1)} %copy-done.2, s32[256]{0:T(256)S(1)} %copy-done.3, s32[2]{0:T(128)S(1)} %pad_add_fusion.me, bf16[64,128,256]{2,1,0:T(8,128)(2,1)S(1)} %get-tuple-element.76.plain, ...), custom_call_target="tpu_custom_call" | custom-call | flops 1000000 | bytes 1048576 | tf_op jit(solution)/shard_map/pallas_call | solution.py:30
  37.3 1.7 %collective-permute-done.11.got = f32[4,8,32,128]{3,2,1,0:T(8,128)S(1)} collective-permute-done((f32[4,8,32,128]{3,2,1,0:T(8,128)S(1)}, f32[4,8,32,128]{3,2,1,0:T(8,128)S(1)}, u32[]{:S(2)}, u32[]{:S(2)}) %collective-permute-start.11) | collective-permute-done | bytes 524320 | tf_op jit(solution)/shard_map/ppermute | solution.py:292
  39.1 1.2 %collective-permute-start.12 = (f32[8,32,128]{2,1,0:T(8,128)S(1)}, f32[8,32,128]{2,1,0:T(8,128)S(1)}, u32[]{:S(2)}, u32[]{:S(2)}) collective-permute-start(f32[8,32,128]{2,1,0:T(8,128)S(1)} %get-tuple-element.92), channel_id=1, source_target_pairs={{0,32},{32,64},{64,96},{96,0},{1,33},{33,65},{65,97},{97,1},{2,34}... | collective-permute-start | bytes 393224 | tf_op jit(solution)/shard_map/ppermute | solution.py:292
  40.3 2.1 %collective-permute-start.13 = (f32[8,32,128]{2,1,0:T(8,128)S(1)}, f32[8,32,128]{2,1,0:T(8,128)S(1)}, u32[]{:S(2)}, u32[]{:S(2)}) collective-permute-start(f32[8,32,128]{2,1,0:T(8,128)S(1)} %get-tuple-element.93), channel_id=1, source_target_pairs={{0,64},{32,96},{64,0},{96,32},{1,65},{33,97},{65,1},{97,33},{2,66}... | collective-permute-start | bytes 393224 | tf_op jit(solution)/shard_map/ppermute | solution.py:292
  43.0 5.9 %collective-permute-start.22 = (f32[32,8,128]{2,1,0:T(8,128)S(1)}, f32[32,8,128]{2,1,0:T(8,128)S(1)}, u32[]{:S(2)}, u32[]{:S(2)}) collective-permute-start(f32[32,8,128]{2,1,0:T(8,128)S(1)} %get-tuple-element.95), channel_id=1, source_target_pairs={{1,0},{2,1},{3,2},{4,3},{5,4},{6,5},{7,6},{8,7},{9,8},{10,9},{11,1... | collective-permute-start | bytes 393224 | tf_op jit(solution)/shard_map/ppermute | solution.py:353
  49.0 1.4 %collective-permute-start.17 = (f32[8,32,128]{2,1,0:T(8,128)S(1)}, f32[8,32,128]{2,1,0:T(8,128)S(1)}, u32[]{:S(2)}, u32[]{:S(2)}) collective-permute-start(f32[8,32,128]{2,1,0:T(8,128)S(1)} %shard_map.82.refs_0_.sent), channel_id=1, source_target_pairs={{0,32},{32,64},{64,96},{96,0},{1,33},{33,65},{65,97},{97,1},{2,34}... | collective-permute-start | bytes 393224 | tf_op jit(solution)/shard_map/ppermute | solution.py:292
  50.4 2.4 %collective-permute-start.16 = (f32[8,32,128]{2,1,0:T(8,128)S(1)}, f32[8,32,128]{2,1,0:T(8,128)S(1)}, u32[]{:S(2)}, u32[]{:S(2)}) collective-permute-start(f32[8,32,128]{2,1,0:T(8,128)S(1)} %shard_map.82.refs_0_.sent), channel_id=1, source_target_pairs={{0,64},{32,96},{64,0},{96,32},{1,65},{33,97},{65,1},{97,33},{2,66}... | collective-permute-start | bytes 393224 | tf_op jit(solution)/shard_map/ppermute | solution.py:292
  52.9 1.2 %collective-permute-start.23 = (f32[32,8,128]{2,1,0:T(8,128)S(1)}, f32[32,8,128]{2,1,0:T(8,128)S(1)}, u32[]{:S(2)}, u32[]{:S(2)}) collective-permute-start(f32[32,8,128]{2,1,0:T(8,128)S(1)} %get-tuple-element.96), channel_id=1, source_target_pairs={{0,1},{1,2},{2,3},{3,4},{4,5},{5,6},{6,7},{7,8},{8,9},{9,10},{10,1... | collective-permute-start | bytes 393224 | tf_op jit(solution)/shard_map/ppermute | solution.py:353
  54.1 1.8 %collective-permute-start.18 = (f32[8,32,128]{2,1,0:T(8,128)S(1)}, f32[8,32,128]{2,1,0:T(8,128)S(1)}, u32[]{:S(2)}, u32[]{:S(2)}) collective-permute-start(f32[8,32,128]{2,1,0:T(8,128)S(1)} %shard_map.82.refs_0_.sent), channel_id=1, source_target_pairs={{0,16},{16,0},{1,17},{17,1},{2,18},{18,2},{3,19},{19,3},{4,20},{20... | collective-permute-start | bytes 393224 | tf_op jit(solution)/shard_map/ppermute | solution.py:292
  55.9 1.2 %collective-permute-start.21 = (f32[8,32,128]{2,1,0:T(8,128)S(1)}, f32[8,32,128]{2,1,0:T(8,128)S(1)}, u32[]{:S(2)}, u32[]{:S(2)}) collective-permute-start(f32[8,32,128]{2,1,0:T(8,128)S(1)} %collective-permute-done.17.refs_3_), channel_id=1, source_target_pairs={{0,16},{16,0},{1,17},{17,1},{2,18},{18,2},{3,19},{19,3},{4,20},{20... | collective-permute-start | bytes 393224 | tf_op jit(solution)/shard_map/ppermute | solution.py:292
  57.1 1.6 %collective-permute-done.16.refs_2_ = f32[8,32,128]{2,1,0:T(8,128)S(1)} collective-permute-done((f32[8,32,128]{2,1,0:T(8,128)S(1)}, f32[8,32,128]{2,1,0:T(8,128)S(1)}, u32[]{:S(2)}, u32[]{:S(2)}) %collective-permute-start.16) | collective-permute-done | bytes 131104 | tf_op jit(solution)/shard_map/ppermute | solution.py:292
  58.7 1.4 %collective-permute-start.20 = (f32[8,32,128]{2,1,0:T(8,128)S(1)}, f32[8,32,128]{2,1,0:T(8,128)S(1)}, u32[]{:S(2)}, u32[]{:S(2)}) collective-permute-start(f32[8,32,128]{2,1,0:T(8,128)S(1)} %collective-permute-done.16.refs_2_), channel_id=1, source_target_pairs={{0,16},{16,0},{1,17},{17,1},{2,18},{18,2},{3,19},{19,3},{4,20},{20... | collective-permute-start | bytes 393224 | tf_op jit(solution)/shard_map/ppermute | solution.py:292
  61.5 6.0 %shard_map.83 = (f32[4,8,32,128]{3,2,1,0:T(8,128)S(1)}, f32[4,8,32,128]{3,2,1,0:T(8,128)S(1)}, f32[32,32,128]{2,1,0:T(8,128)}, f32[2,8,128]{2,1,0:T(8,128)S(1)},...) custom-call(s32[256]{0:T(256)S(1)} %copy-done.2, s32[256]{0:T(256)S(1)} %copy-done.3, s32[2]{0:T(128)S(1)} %pad_add_fusion.me, ...), custom_call_target="tpu_custom_call" | custom-call | flops 1000000 | bytes 1048576 | tf_op jit(solution)/shard_map/pallas_call | solution.py:30
  67.5 2.2 %collective-permute-start.24 = (f32[4,8,32,128]{3,2,1,0:T(8,128)S(1)}, f32[4,8,32,128]{3,2,1,0:T(8,128)S(1)}, u32[]{:S(2)}, u32[]{:S(2)}) collective-permute-start(f32[4,8,32,128]{3,2,1,0:T(8,128)S(1)} %get-tuple-element.107), channel_id=1, source_target_pairs={{0,16},{16,0},{1,17},{17,1},{2,18},{18,2},{3,19},{19,3},{4,20},{20... | collective-permute-start | bytes 1572872 | tf_op jit(solution)/shard_map/ppermute | solution.py:292
  69.7 1.5 %collective-permute-done.24.got = f32[4,8,32,128]{3,2,1,0:T(8,128)S(1)} collective-permute-done((f32[4,8,32,128]{3,2,1,0:T(8,128)S(1)}, f32[4,8,32,128]{3,2,1,0:T(8,128)S(1)}, u32[]{:S(2)}, u32[]{:S(2)}) %collective-permute-start.24) | collective-permute-done | bytes 524320 | tf_op jit(solution)/shard_map/ppermute | solution.py:292
  71.3 1.4 %collective-permute-start.25 = (f32[8,32,128]{2,1,0:T(8,128)S(1)}, f32[8,32,128]{2,1,0:T(8,128)S(1)}, u32[]{:S(2)}, u32[]{:S(2)}) collective-permute-start(f32[8,32,128]{2,1,0:T(8,128)S(1)} %get-tuple-element.109), channel_id=1, source_target_pairs={{0,32},{32,64},{64,96},{96,0},{1,33},{33,65},{65,97},{97,1},{2,34}... | collective-permute-start | bytes 393224 | tf_op jit(solution)/shard_map/ppermute | solution.py:292
  73.1 2.0 %collective-permute-start.27 = (f32[8,32,128]{2,1,0:T(8,128)S(1)}, f32[8,32,128]{2,1,0:T(8,128)S(1)}, u32[]{:S(2)}, u32[]{:S(2)}) collective-permute-start(f32[8,32,128]{2,1,0:T(8,128)S(1)} %get-tuple-element.111), channel_id=1, source_target_pairs={{0,96},{32,0},{64,32},{96,64},{1,97},{33,1},{65,33},{97,65},{2,98}... | collective-permute-start | bytes 393224 | tf_op jit(solution)/shard_map/ppermute | solution.py:292
  75.1 3.3 %collective-permute-start.28 = (f32[32,8,128]{2,1,0:T(8,128)S(1)}, f32[32,8,128]{2,1,0:T(8,128)S(1)}, u32[]{:S(2)}, u32[]{:S(2)}) collective-permute-start(f32[32,8,128]{2,1,0:T(8,128)S(1)} %get-tuple-element.125), channel_id=1, source_target_pairs={{1,0},{2,1},{3,2},{4,3},{5,4},{6,5},{7,6},{8,7},{9,8},{10,9},{11,1... | collective-permute-start | bytes 393224 | tf_op jit(solution)/shard_map/ppermute | solution.py:367
  79.2 1.2 %collective-permute-done.27.c = f32[8,32,128]{2,1,0:T(8,128)S(1)} collective-permute-done((f32[8,32,128]{2,1,0:T(8,128)S(1)}, f32[8,32,128]{2,1,0:T(8,128)S(1)}, u32[]{:S(2)}, u32[]{:S(2)}) %collective-permute-start.27) | collective-permute-done | bytes 131104 | tf_op jit(solution)/shard_map/ppermute | solution.py:292
  81.5 18.8 %all_to_all.20 = f32[128,1,128]{2,1,0:T(1,128)S(1)} all-to-all(f32[128,1,128]{2,1,0:T(1,128)S(1)} %bitcast.16), channel_id=1, replica_groups=mesh['tile_0'=4,'tile_1'=2,'slab_0'=4,'slab_1'=4] {'tile_0','tile_1','sl..., dimensions={0} | all-to-all | bytes 131072 | tf_op jit(solution)/shard_map/all_to_all | solution.py:310
  101.8 2.7 %shard_map.88 = (f32[32,4096]{1,0:T(8,128)}, f32[32,1024]{1,0:T(8,128)}) custom-call(s32[2]{0:T(128)S(1)} %add_convert_fusion.ends, f32[2]{0:T(128)S(1)} %get-tuple-element.128.alphas, f32[32,4096]{1,0:T(8,128)S(1)} %copy-done, f32[32,32,128]{2,1,0:T(8,128)S(1)} %get-tuple-element.105.refs_8_.grad, f32[32,32,128]{2,1,0:T(8,128)} %get-tuple-element.122.turned, ...), custom_call_target="tpu_custom_call" | custom-call | flops 1000000 | bytes 1048576 | tf_op jit(solution)/shard_map/pallas_call | solution.py:30
  (56 shorter events, 10.1 us)
Async XLA Ops:
  0.6 31.0 %copy-start.3 = (s32[256]{0:T(256)S(1)}, s32[256]{0:T(256)}, u32[]{:S(2)}) copy-start(s32[256]{0:T(256)} %strips.3) | copy-start | bytes 3076
  6.5 3.0 %collective-permute-start = (f32[4,8,32,128]{3,2,1,0:T(8,128)S(1)}, f32[4,8,32,128]{3,2,1,0:T(8,128)S(1)}, u32[]{:S(2)}, u32[]{:S(2)}) collective-permute-start(f32[4,8,32,128]{3,2,1,0:T(8,128)S(1)} %get-tuple-element.79), channel_id=1, source_target_pairs={{0,16},{16,0},{1,17},{17,1},{2,18},{18,2},{3,19},{19,3},{4,20},{20... | collective-permute-start | bytes 1572872 | tf_op jit(solution)/shard_map/ppermute | solution.py:292
  9.5 6.3 %collective-permute-start.1 = (f32[8,32,128]{2,1,0:T(8,128)S(1)}, f32[8,32,128]{2,1,0:T(8,128)S(1)}, u32[]{:S(2)}, u32[]{:S(2)}) collective-permute-start(f32[8,32,128]{2,1,0:T(8,128)S(1)} %get-tuple-element.81), channel_id=1, source_target_pairs={{0,32},{32,64},{64,96},{96,0},{1,33},{33,65},{65,97},{97,1},{2,34}... | collective-permute-start | bytes 393224 | tf_op jit(solution)/shard_map/ppermute | solution.py:292
  11.0 8.7 %collective-permute-start.2 = (f32[8,32,128]{2,1,0:T(8,128)S(1)}, f32[8,32,128]{2,1,0:T(8,128)S(1)}, u32[]{:S(2)}, u32[]{:S(2)}) collective-permute-start(f32[8,32,128]{2,1,0:T(8,128)S(1)} %get-tuple-element.82), channel_id=1, source_target_pairs={{0,64},{32,96},{64,0},{96,32},{1,65},{33,97},{65,1},{97,33},{2,66}... | collective-permute-start | bytes 393224 | tf_op jit(solution)/shard_map/ppermute | solution.py:292
  13.6 6.0 %collective-permute-start.3 = (f32[8,32,128]{2,1,0:T(8,128)S(1)}, f32[8,32,128]{2,1,0:T(8,128)S(1)}, u32[]{:S(2)}, u32[]{:S(2)}) collective-permute-start(f32[8,32,128]{2,1,0:T(8,128)S(1)} %get-tuple-element.83), channel_id=1, source_target_pairs={{0,96},{32,0},{64,32},{96,64},{1,97},{33,1},{65,33},{97,65},{2,98}... | collective-permute-start | bytes 393224 | tf_op jit(solution)/shard_map/ppermute | solution.py:292
  19.7 6.5 %collective-permute-start.6 = (f32[8,32,128]{2,1,0:T(8,128)S(1)}, f32[8,32,128]{2,1,0:T(8,128)S(1)}, u32[]{:S(2)}, u32[]{:S(2)}) collective-permute-start(f32[8,32,128]{2,1,0:T(8,128)S(1)} %get-tuple-element.84.refs_0_), channel_id=1, source_target_pairs={{0,32},{32,64},{64,96},{96,0},{1,33},{33,65},{65,97},{97,1},{2,34}... | collective-permute-start | bytes 393224 | tf_op jit(solution)/shard_map/ppermute | solution.py:292
  20.8 7.6 %collective-permute-start.5 = (f32[8,32,128]{2,1,0:T(8,128)S(1)}, f32[8,32,128]{2,1,0:T(8,128)S(1)}, u32[]{:S(2)}, u32[]{:S(2)}) collective-permute-start(f32[8,32,128]{2,1,0:T(8,128)S(1)} %get-tuple-element.84.refs_0_), channel_id=1, source_target_pairs={{0,64},{32,96},{64,0},{96,32},{1,65},{33,97},{65,1},{97,33},{2,66}... | collective-permute-start | bytes 393224 | tf_op jit(solution)/shard_map/ppermute | solution.py:292
  23.0 7.3 %collective-permute-start.4 = (f32[8,32,128]{2,1,0:T(8,128)S(1)}, f32[8,32,128]{2,1,0:T(8,128)S(1)}, u32[]{:S(2)}, u32[]{:S(2)}) collective-permute-start(f32[8,32,128]{2,1,0:T(8,128)S(1)} %get-tuple-element.84.refs_0_), channel_id=1, source_target_pairs={{0,96},{32,0},{64,32},{96,64},{1,97},{33,1},{65,33},{97,65},{2,98}... | collective-permute-start | bytes 393224 | tf_op jit(solution)/shard_map/ppermute | solution.py:292
  23.9 6.4 %collective-permute-start.7 = (f32[8,32,128]{2,1,0:T(8,128)S(1)}, f32[8,32,128]{2,1,0:T(8,128)S(1)}, u32[]{:S(2)}, u32[]{:S(2)}) collective-permute-start(f32[8,32,128]{2,1,0:T(8,128)S(1)} %get-tuple-element.84.refs_0_), channel_id=1, source_target_pairs={{0,16},{16,0},{1,17},{17,1},{2,18},{18,2},{3,19},{19,3},{4,20},{20... | collective-permute-start | bytes 393224 | tf_op jit(solution)/shard_map/ppermute | solution.py:292
  26.2 4.1 %collective-permute-start.10 = (f32[8,32,128]{2,1,0:T(8,128)S(1)}, f32[8,32,128]{2,1,0:T(8,128)S(1)}, u32[]{:S(2)}, u32[]{:S(2)}) collective-permute-start(f32[8,32,128]{2,1,0:T(8,128)S(1)} %collective-permute-done.6.refs_3_), channel_id=1, source_target_pairs={{0,16},{16,0},{1,17},{17,1},{2,18},{18,2},{3,19},{19,3},{4,20},{20... | collective-permute-start | bytes 393224 | tf_op jit(solution)/shard_map/ppermute | solution.py:292
  28.4 2.9 %collective-permute-start.9 = (f32[8,32,128]{2,1,0:T(8,128)S(1)}, f32[8,32,128]{2,1,0:T(8,128)S(1)}, u32[]{:S(2)}, u32[]{:S(2)}) collective-permute-start(f32[8,32,128]{2,1,0:T(8,128)S(1)} %collective-permute-done.5.refs_2_), channel_id=1, source_target_pairs={{0,16},{16,0},{1,17},{17,1},{2,18},{18,2},{3,19},{19,3},{4,20},{20... | collective-permute-start | bytes 393224 | tf_op jit(solution)/shard_map/ppermute | solution.py:292
  30.3 1.3 %collective-permute-start.8 = (f32[8,32,128]{2,1,0:T(8,128)S(1)}, f32[8,32,128]{2,1,0:T(8,128)S(1)}, u32[]{:S(2)}, u32[]{:S(2)}) collective-permute-start(f32[8,32,128]{2,1,0:T(8,128)S(1)} %collective-permute-done.4.refs_1_), channel_id=1, source_target_pairs={{0,16},{16,0},{1,17},{17,1},{2,18},{18,2},{3,19},{19,3},{4,20},{20... | collective-permute-start | bytes 393224 | tf_op jit(solution)/shard_map/ppermute | solution.py:292
  37.1 2.0 %collective-permute-start.11 = (f32[4,8,32,128]{3,2,1,0:T(8,128)S(1)}, f32[4,8,32,128]{3,2,1,0:T(8,128)S(1)}, u32[]{:S(2)}, u32[]{:S(2)}) collective-permute-start(f32[4,8,32,128]{3,2,1,0:T(8,128)S(1)} %get-tuple-element.90), channel_id=1, source_target_pairs={{0,16},{16,0},{1,17},{17,1},{2,18},{18,2},{3,19},{19,3},{4,20},{20... | collective-permute-start | bytes 1572872 | tf_op jit(solution)/shard_map/ppermute | solution.py:292
  39.1 9.8 %collective-permute-start.12 = (f32[8,32,128]{2,1,0:T(8,128)S(1)}, f32[8,32,128]{2,1,0:T(8,128)S(1)}, u32[]{:S(2)}, u32[]{:S(2)}) collective-permute-start(f32[8,32,128]{2,1,0:T(8,128)S(1)} %get-tuple-element.92), channel_id=1, source_target_pairs={{0,32},{32,64},{64,96},{96,0},{1,33},{33,65},{65,97},{97,1},{2,34}... | collective-permute-start | bytes 393224 | tf_op jit(solution)/shard_map/ppermute | solution.py:292
  40.3 8.6 %collective-permute-start.13 = (f32[8,32,128]{2,1,0:T(8,128)S(1)}, f32[8,32,128]{2,1,0:T(8,128)S(1)}, u32[]{:S(2)}, u32[]{:S(2)}) collective-permute-start(f32[8,32,128]{2,1,0:T(8,128)S(1)} %get-tuple-element.93), channel_id=1, source_target_pairs={{0,64},{32,96},{64,0},{96,32},{1,65},{33,97},{65,1},{97,33},{2,66}... | collective-permute-start | bytes 393224 | tf_op jit(solution)/shard_map/ppermute | solution.py:292
  42.4 6.5 %collective-permute-start.14 = (f32[8,32,128]{2,1,0:T(8,128)S(1)}, f32[8,32,128]{2,1,0:T(8,128)S(1)}, u32[]{:S(2)}, u32[]{:S(2)}) collective-permute-start(f32[8,32,128]{2,1,0:T(8,128)S(1)} %get-tuple-element.94), channel_id=1, source_target_pairs={{0,96},{32,0},{64,32},{96,64},{1,97},{33,1},{65,33},{97,65},{2,98}... | collective-permute-start | bytes 393224 | tf_op jit(solution)/shard_map/ppermute | solution.py:292
  43.0 11.1 %collective-permute-start.22 = (f32[32,8,128]{2,1,0:T(8,128)S(1)}, f32[32,8,128]{2,1,0:T(8,128)S(1)}, u32[]{:S(2)}, u32[]{:S(2)}) collective-permute-start(f32[32,8,128]{2,1,0:T(8,128)S(1)} %get-tuple-element.95), channel_id=1, source_target_pairs={{1,0},{2,1},{3,2},{4,3},{5,4},{6,5},{7,6},{8,7},{9,8},{10,9},{11,1... | collective-permute-start | bytes 393224 | tf_op jit(solution)/shard_map/ppermute | solution.py:353
  49.0 7.0 %collective-permute-start.17 = (f32[8,32,128]{2,1,0:T(8,128)S(1)}, f32[8,32,128]{2,1,0:T(8,128)S(1)}, u32[]{:S(2)}, u32[]{:S(2)}) collective-permute-start(f32[8,32,128]{2,1,0:T(8,128)S(1)} %shard_map.82.refs_0_.sent), channel_id=1, source_target_pairs={{0,32},{32,64},{64,96},{96,0},{1,33},{33,65},{65,97},{97,1},{2,34}... | collective-permute-start | bytes 393224 | tf_op jit(solution)/shard_map/ppermute | solution.py:292
  50.4 8.3 %collective-permute-start.16 = (f32[8,32,128]{2,1,0:T(8,128)S(1)}, f32[8,32,128]{2,1,0:T(8,128)S(1)}, u32[]{:S(2)}, u32[]{:S(2)}) collective-permute-start(f32[8,32,128]{2,1,0:T(8,128)S(1)} %shard_map.82.refs_0_.sent), channel_id=1, source_target_pairs={{0,64},{32,96},{64,0},{96,32},{1,65},{33,97},{65,1},{97,33},{2,66}... | collective-permute-start | bytes 393224 | tf_op jit(solution)/shard_map/ppermute | solution.py:292
  52.9 7.3 %collective-permute-start.15 = (f32[8,32,128]{2,1,0:T(8,128)S(1)}, f32[8,32,128]{2,1,0:T(8,128)S(1)}, u32[]{:S(2)}, u32[]{:S(2)}) collective-permute-start(f32[8,32,128]{2,1,0:T(8,128)S(1)} %shard_map.82.refs_0_.sent), channel_id=1, source_target_pairs={{0,96},{32,0},{64,32},{96,64},{1,97},{33,1},{65,33},{97,65},{2,98}... | collective-permute-start | bytes 393224 | tf_op jit(solution)/shard_map/ppermute | solution.py:292
  52.9 8.3 %collective-permute-start.23 = (f32[32,8,128]{2,1,0:T(8,128)S(1)}, f32[32,8,128]{2,1,0:T(8,128)S(1)}, u32[]{:S(2)}, u32[]{:S(2)}) collective-permute-start(f32[32,8,128]{2,1,0:T(8,128)S(1)} %get-tuple-element.96), channel_id=1, source_target_pairs={{0,1},{1,2},{2,3},{3,4},{4,5},{5,6},{6,7},{7,8},{8,9},{9,10},{10,1... | collective-permute-start | bytes 393224 | tf_op jit(solution)/shard_map/ppermute | solution.py:353
  54.1 7.1 %collective-permute-start.18 = (f32[8,32,128]{2,1,0:T(8,128)S(1)}, f32[8,32,128]{2,1,0:T(8,128)S(1)}, u32[]{:S(2)}, u32[]{:S(2)}) collective-permute-start(f32[8,32,128]{2,1,0:T(8,128)S(1)} %shard_map.82.refs_0_.sent), channel_id=1, source_target_pairs={{0,16},{16,0},{1,17},{17,1},{2,18},{18,2},{3,19},{19,3},{4,20},{20... | collective-permute-start | bytes 393224 | tf_op jit(solution)/shard_map/ppermute | solution.py:292
  55.9 5.3 %collective-permute-start.21 = (f32[8,32,128]{2,1,0:T(8,128)S(1)}, f32[8,32,128]{2,1,0:T(8,128)S(1)}, u32[]{:S(2)}, u32[]{:S(2)}) collective-permute-start(f32[8,32,128]{2,1,0:T(8,128)S(1)} %collective-permute-done.17.refs_3_), channel_id=1, source_target_pairs={{0,16},{16,0},{1,17},{17,1},{2,18},{18,2},{3,19},{19,3},{4,20},{20... | collective-permute-start | bytes 393224 | tf_op jit(solution)/shard_map/ppermute | solution.py:292
  58.7 2.5 %collective-permute-start.20 = (f32[8,32,128]{2,1,0:T(8,128)S(1)}, f32[8,32,128]{2,1,0:T(8,128)S(1)}, u32[]{:S(2)}, u32[]{:S(2)}) collective-permute-start(f32[8,32,128]{2,1,0:T(8,128)S(1)} %collective-permute-done.16.refs_2_), channel_id=1, source_target_pairs={{0,16},{16,0},{1,17},{17,1},{2,18},{18,2},{3,19},{19,3},{4,20},{20... | collective-permute-start | bytes 393224 | tf_op jit(solution)/shard_map/ppermute | solution.py:292
  60.1 1.3 %collective-permute-start.19 = (f32[8,32,128]{2,1,0:T(8,128)S(1)}, f32[8,32,128]{2,1,0:T(8,128)S(1)}, u32[]{:S(2)}, u32[]{:S(2)}) collective-permute-start(f32[8,32,128]{2,1,0:T(8,128)S(1)} %collective-permute-done.15.refs_1_), channel_id=1, source_target_pairs={{0,16},{16,0},{1,17},{17,1},{2,18},{18,2},{3,19},{19,3},{4,20},{20... | collective-permute-start | bytes 393224 | tf_op jit(solution)/shard_map/ppermute | solution.py:292
  67.5 34.3 %copy-start = (f32[32,4096]{1,0:T(8,128)S(1)}, f32[32,4096]{1,0:T(8,128)}, u32[]{:S(2)}) copy-start(f32[32,4096]{1,0:T(8,128)} %volume.1) | copy-start | bytes 1572868
  67.5 3.7 %collective-permute-start.24 = (f32[4,8,32,128]{3,2,1,0:T(8,128)S(1)}, f32[4,8,32,128]{3,2,1,0:T(8,128)S(1)}, u32[]{:S(2)}, u32[]{:S(2)}) collective-permute-start(f32[4,8,32,128]{3,2,1,0:T(8,128)S(1)} %get-tuple-element.107), channel_id=1, source_target_pairs={{0,16},{16,0},{1,17},{17,1},{2,18},{18,2},{3,19},{19,3},{4,20},{20... | collective-permute-start | bytes 1572872 | tf_op jit(solution)/shard_map/ppermute | solution.py:292
  71.3 7.3 %collective-permute-start.25 = (f32[8,32,128]{2,1,0:T(8,128)S(1)}, f32[8,32,128]{2,1,0:T(8,128)S(1)}, u32[]{:S(2)}, u32[]{:S(2)}) collective-permute-start(f32[8,32,128]{2,1,0:T(8,128)S(1)} %get-tuple-element.109), channel_id=1, source_target_pairs={{0,32},{32,64},{64,96},{96,0},{1,33},{33,65},{65,97},{97,1},{2,34}... | collective-permute-start | bytes 393224 | tf_op jit(solution)/shard_map/ppermute | solution.py:292
  72.7 6.5 %collective-permute-start.26 = (f32[8,32,128]{2,1,0:T(8,128)S(1)}, f32[8,32,128]{2,1,0:T(8,128)S(1)}, u32[]{:S(2)}, u32[]{:S(2)}) collective-permute-start(f32[8,32,128]{2,1,0:T(8,128)S(1)} %get-tuple-element.110), channel_id=1, source_target_pairs={{0,64},{32,96},{64,0},{96,32},{1,65},{33,97},{65,1},{97,33},{2,66}... | collective-permute-start | bytes 393224 | tf_op jit(solution)/shard_map/ppermute | solution.py:292
  73.1 7.2 %collective-permute-start.27 = (f32[8,32,128]{2,1,0:T(8,128)S(1)}, f32[8,32,128]{2,1,0:T(8,128)S(1)}, u32[]{:S(2)}, u32[]{:S(2)}) collective-permute-start(f32[8,32,128]{2,1,0:T(8,128)S(1)} %get-tuple-element.111), channel_id=1, source_target_pairs={{0,96},{32,0},{64,32},{96,64},{1,97},{33,1},{65,33},{97,65},{2,98}... | collective-permute-start | bytes 393224 | tf_op jit(solution)/shard_map/ppermute | solution.py:292
  75.1 26.6 %collective-permute-start.28 = (f32[32,8,128]{2,1,0:T(8,128)S(1)}, f32[32,8,128]{2,1,0:T(8,128)S(1)}, u32[]{:S(2)}, u32[]{:S(2)}) collective-permute-start(f32[32,8,128]{2,1,0:T(8,128)S(1)} %get-tuple-element.125), channel_id=1, source_target_pairs={{1,0},{2,1},{3,2},{4,3},{5,4},{6,5},{7,6},{8,7},{9,8},{10,9},{11,1... | collective-permute-start | bytes 393224 | tf_op jit(solution)/shard_map/ppermute | solution.py:367
  78.4 23.3 %collective-permute-start.29 = (f32[32,8,128]{2,1,0:T(8,128)S(1)}, f32[32,8,128]{2,1,0:T(8,128)S(1)}, u32[]{:S(2)}, u32[]{:S(2)}) collective-permute-start(f32[32,8,128]{2,1,0:T(8,128)S(1)} %get-tuple-element.126), channel_id=1, source_target_pairs={{0,1},{1,2},{2,3},{3,4},{4,5},{5,6},{6,7},{7,8},{8,9},{9,10},{10,1... | collective-permute-start | bytes 393224 | tf_op jit(solution)/shard_map/ppermute | solution.py:367
  (4 other events, 92.2 us)
